TPU v7x, 128 devices: a whole 4x4x4 slice. The times are simulated.
128 devices in a mesh: hp: 4 (over x), cp: 32 (over z, y, core).
Axes of the slice: x: 4, y: 4, z: 4, core: 2. Of those that a mesh axis runs over, the one named last changes fastest.
Arguments:
- q: bfloat16 [1, 16384, 32, 128], P(None, ('cp', 'hp'))
- k: bfloat16 [1, 16384, 32, 128], P(None, ('cp', 'hp'))
- v: bfloat16 [1, 16384, 32, 128], P(None, ('cp', 'hp'))
- o: bfloat16 [1, 16384, 32, 128], P(None, ('cp', 'hp'))
- do: bfloat16 [1, 16384, 32, 128], P(None, ('cp', 'hp'))
- lse: float32 [1, 32, 16384], P(None, None, ('cp', 'hp'))
Outputs:
- output 1: bfloat16 [1, 16384, 32, 128], P(None, ('cp', 'hp'))
- output 2: bfloat16 [1, 16384, 32, 128], P(None, ('cp', 'hp'))
- output 3: bfloat16 [1, 16384, 32, 128], P(None, ('cp', 'hp'))
All inputs are finite; a program needn't handle non-finite values.
Results may differ from a plain program's by a relative error of at most 0.001.
Values are sent between devices in bfloat16 or wider.
A program may use at most 1 GiB of HBM per device.

v0:
```python
import jax
import jax.numpy as jnp
from jax import lax
from jax.sharding import PartitionSpec as P


def _block(q, do, lse, dlt, k, v, mask, scale):
    s = jnp.einsum('bqhgd,bkhd->bhgqk', q, k, preferred_element_type=jnp.float32) * scale
    p = jnp.exp(s - lse[..., None])
    if mask is not None:
        p = jnp.where(mask, p, 0.0)
    dv = jnp.einsum('bhgqk,bqhgd->bkhd', p.astype(jnp.bfloat16), do, preferred_element_type=jnp.float32)
    dp = jnp.einsum('bqhgd,bkhd->bhgqk', do, v, preferred_element_type=jnp.float32)
    ds = (p * (dp - dlt[..., None])).astype(jnp.bfloat16)
    dq = jnp.einsum('bhgqk,bkhd->bqhgd', ds, k, preferred_element_type=jnp.float32) * scale
    dk = jnp.einsum('bhgqk,bqhgd->bkhd', ds, q, preferred_element_type=jnp.float32) * scale
    return dq, dk, dv


def _own_step(q, do, lse, dlt, k, v, scale):
    c = q.shape[1] // 2
    tri = jnp.tril(jnp.ones((c, c), jnp.bool_))
    dq0, dk0, dv0 = _block(q[:, :c], do[:, :c], lse[..., :c], dlt[..., :c], k[:, :c], v[:, :c], tri, scale)
    m1 = jnp.concatenate([jnp.ones((c, c), jnp.bool_), tri], axis=1)
    dq1, dk1, dv1 = _block(q[:, c:], do[:, c:], lse[..., c:], dlt[..., c:], k, v, m1, scale)
    z = jnp.zeros_like(dk0)
    return (jnp.concatenate([dq0, dq1], axis=1), dk1 + jnp.concatenate([dk0, z], axis=1), dv1 + jnp.concatenate([dv0, z], axis=1))


def _remote_step(earlier, q, do, lse, dlt, k, v, scale):
    c = q.shape[1] // 2

    def first(ops):
        q, do, lse, dlt, k, v = ops
        dq, dk0, dv0 = _block(q, do, lse, dlt, k[:, :c], v[:, :c], None, scale)
        z = jnp.zeros_like(dk0)
        return dq, jnp.concatenate([dk0, z], axis=1), jnp.concatenate([dv0, z], axis=1)

    def second(ops):
        q, do, lse, dlt, k, v = ops
        dq1, dk, dv = _block(q[:, c:], do[:, c:], lse[..., c:], dlt[..., c:], k, v, None, scale)
        return jnp.concatenate([jnp.zeros_like(dq1), dq1], axis=1), dk, dv

    return lax.cond(earlier, first, second, (q, do, lse, dlt, k, v))


def solution(mesh):
    cp = mesh.shape['cp']
    seq = P(None, ('cp', 'hp'), None, None)
    stat = P(None, None, ('cp', 'hp'))
    perm = [(r, (r + 1) % cp) for r in range(cp)]

    def body(q, k, v, o, do, lse):
        i = lax.axis_index('cp')
        b, _, hq, d = q.shape
        scale = d ** -0.5
        dlt = jnp.sum(do.astype(jnp.float32) * o.astype(jnp.float32), axis=-1).transpose(0, 2, 1)
        st = lax.all_to_all(jnp.stack([lse, dlt]), 'hp', 2, 3, tiled=True)
        q, k, v, do = [lax.all_to_all(x, 'hp', 2, 1, tiled=True) for x in (q, k, v, do)]
        t, hk = k.shape[1], k.shape[2]
        g = q.shape[2] // hk
        q = q.reshape(b, t, hk, g, d)
        do = do.reshape(b, t, hk, g, d)
        lse_l = st[0].reshape(b, hk, g, t)
        dlt_l = st[1].reshape(b, hk, g, t)
        dq, dk, dv = _own_step(q, do, lse_l, dlt_l, k, v, scale)
        for s in range(1, cp):
            k, v, dk, dv = [lax.ppermute(x, 'cp', perm) for x in (k, v, dk, dv)]
            ddq, ddk, ddv = _remote_step(s <= i, q, do, lse_l, dlt_l, k, v, scale)
            dq, dk, dv = dq + ddq, dk + ddk, dv + ddv
        dk, dv = [lax.ppermute(x, 'cp', perm) for x in (dk, dv)]
        dq = dq.reshape(b, t, hk * g, d)
        return tuple(lax.all_to_all(x.astype(jnp.bfloat16), 'hp', 1, 2, tiled=True) for x in (dq, dk, dv))

    return jax.shard_map(body, mesh=mesh, in_specs=(seq, seq, seq, seq, seq, stat), out_specs=(seq, seq, seq), check_vma=False)
```

profile of v0, /device:TPU:120, one launch (start us, length us, event | category | flops | bytes accessed | tf_op | source)
XLA Modules:
  0.0 2757.3 jit_solution(9372018562530470540)
XLA Ops:
  144.5 29.9 %collective-permute-done.2 = bf16[1,512,8,128]{3,1,2,0:T(8,128)(2,1)S(1)} collective-permute-done((bf16[1,512,8,128]{3,1,2,0:T(8,128)(2,1)}, bf16[1,512,8,128]{3,1,2,0:T(8,128)(2,1)S(1)}, u32[]{:S(2)}, u32[]{:S(2)}) %collective-permute-start.2) | collective-permute-done | bytes 1048608 | tf_op jit(solution)/shard_map/ppermute | solution.py:68
  198.8 43.0 %collective-permute-done.4 = bf16[1,512,8,128]{3,1,2,0:T(8,128)(2,1)} collective-permute-done((bf16[1,512,8,128]{3,1,2,0:T(8,128)(2,1)S(1)}, bf16[1,512,8,128]{3,1,2,0:T(8,128)(2,1)}, u32[]{:S(2)}, u32[]{:S(2)}) %collective-permute-start.4) | collective-permute-done | bytes 1048608 | tf_op jit(solution)/shard_map/ppermute | solution.py:68
  272.2 53.3 %collective-permute-done.6 = bf16[1,512,8,128]{3,1,2,0:T(8,128)(2,1)S(1)} collective-permute-done((bf16[1,512,8,128]{3,1,2,0:T(8,128)(2,1)}, bf16[1,512,8,128]{3,1,2,0:T(8,128)(2,1)S(1)}, u32[]{:S(2)}, u32[]{:S(2)}) %collective-permute-start.6) | collective-permute-done | bytes 1048608 | tf_op jit(solution)/shard_map/ppermute | solution.py:68
  356.9 50.1 %collective-permute-done.8 = bf16[1,512,8,128]{3,1,2,0:T(8,128)(2,1)} collective-permute-done((bf16[1,512,8,128]{3,1,2,0:T(8,128)(2,1)S(1)}, bf16[1,512,8,128]{3,1,2,0:T(8,128)(2,1)}, u32[]{:S(2)}, u32[]{:S(2)}) %collective-permute-start.8) | collective-permute-done | bytes 1048608 | tf_op jit(solution)/shard_map/ppermute | solution.py:68
  444.2 46.7 %collective-permute-done.10 = bf16[1,512,8,128]{3,1,2,0:T(8,128)(2,1)S(1)} collective-permute-done((bf16[1,512,8,128]{3,1,2,0:T(8,128)(2,1)}, bf16[1,512,8,128]{3,1,2,0:T(8,128)(2,1)S(1)}, u32[]{:S(2)}, u32[]{:S(2)}) %collective-permute-start.10) | collective-permute-done | bytes 1048608 | tf_op jit(solution)/shard_map/ppermute | solution.py:68
  528.9 43.4 %collective-permute-done.12 = bf16[1,512,8,128]{3,1,2,0:T(8,128)(2,1)} collective-permute-done((bf16[1,512,8,128]{3,1,2,0:T(8,128)(2,1)S(1)}, bf16[1,512,8,128]{3,1,2,0:T(8,128)(2,1)}, u32[]{:S(2)}, u32[]{:S(2)}) %collective-permute-start.12) | collective-permute-done | bytes 1048608 | tf_op jit(solution)/shard_map/ppermute | solution.py:68
  616.1 39.9 %collective-permute-done.14 = bf16[1,512,8,128]{3,1,2,0:T(8,128)(2,1)S(1)} collective-permute-done((bf16[1,512,8,128]{3,1,2,0:T(8,128)(2,1)}, bf16[1,512,8,128]{3,1,2,0:T(8,128)(2,1)S(1)}, u32[]{:S(2)}, u32[]{:S(2)}) %collective-permute-start.14) | collective-permute-done | bytes 1048608 | tf_op jit(solution)/shard_map/ppermute | solution.py:68
  701.0 36.7 %collective-permute-done.16 = bf16[1,512,8,128]{3,1,2,0:T(8,128)(2,1)} collective-permute-done((bf16[1,512,8,128]{3,1,2,0:T(8,128)(2,1)S(1)}, bf16[1,512,8,128]{3,1,2,0:T(8,128)(2,1)}, u32[]{:S(2)}, u32[]{:S(2)}) %collective-permute-start.16) | collective-permute-done | bytes 1048608 | tf_op jit(solution)/shard_map/ppermute | solution.py:68
  788.1 33.2 %collective-permute-done.18 = bf16[1,512,8,128]{3,1,2,0:T(8,128)(2,1)S(1)} collective-permute-done((bf16[1,512,8,128]{3,1,2,0:T(8,128)(2,1)}, bf16[1,512,8,128]{3,1,2,0:T(8,128)(2,1)S(1)}, u32[]{:S(2)}, u32[]{:S(2)}) %collective-permute-start.18) | collective-permute-done | bytes 1048608 | tf_op jit(solution)/shard_map/ppermute | solution.py:68
  872.8 31.0 %collective-permute-done.20 = bf16[1,512,8,128]{3,1,2,0:T(8,128)(2,1)} collective-permute-done((bf16[1,512,8,128]{3,1,2,0:T(8,128)(2,1)S(1)}, bf16[1,512,8,128]{3,1,2,0:T(8,128)(2,1)}, u32[]{:S(2)}, u32[]{:S(2)}) %collective-permute-start.20) | collective-permute-done | bytes 1048608 | tf_op jit(solution)/shard_map/ppermute | solution.py:68
  960.2 30.6 %collective-permute-done.22 = bf16[1,512,8,128]{3,1,2,0:T(8,128)(2,1)S(1)} collective-permute-done((bf16[1,512,8,128]{3,1,2,0:T(8,128)(2,1)}, bf16[1,512,8,128]{3,1,2,0:T(8,128)(2,1)S(1)}, u32[]{:S(2)}, u32[]{:S(2)}) %collective-permute-start.22) | collective-permute-done | bytes 1048608 | tf_op jit(solution)/shard_map/ppermute | solution.py:68
  1044.9 31.0 %collective-permute-done.24 = bf16[1,512,8,128]{3,1,2,0:T(8,128)(2,1)} collective-permute-done((bf16[1,512,8,128]{3,1,2,0:T(8,128)(2,1)S(1)}, bf16[1,512,8,128]{3,1,2,0:T(8,128)(2,1)}, u32[]{:S(2)}, u32[]{:S(2)}) %collective-permute-start.24) | collective-permute-done | bytes 1048608 | tf_op jit(solution)/shard_map/ppermute | solution.py:68
  1131.9 30.6 %collective-permute-done.26 = bf16[1,512,8,128]{3,1,2,0:T(8,128)(2,1)S(1)} collective-permute-done((bf16[1,512,8,128]{3,1,2,0:T(8,128)(2,1)}, bf16[1,512,8,128]{3,1,2,0:T(8,128)(2,1)S(1)}, u32[]{:S(2)}, u32[]{:S(2)}) %collective-permute-start.26) | collective-permute-done | bytes 1048608 | tf_op jit(solution)/shard_map/ppermute | solution.py:68
  1185.1 22.8 collective-permute-start.75
  1216.8 31.0 %collective-permute-done.28 = bf16[1,512,8,128]{3,1,2,0:T(8,128)(2,1)} collective-permute-done((bf16[1,512,8,128]{3,1,2,0:T(8,128)(2,1)S(1)}, bf16[1,512,8,128]{3,1,2,0:T(8,128)(2,1)}, u32[]{:S(2)}, u32[]{:S(2)}) %collective-permute-start.28) | collective-permute-done | bytes 1048608 | tf_op jit(solution)/shard_map/ppermute | solution.py:68
  1303.9 30.6 %collective-permute-done.30 = bf16[1,512,8,128]{3,1,2,0:T(8,128)(2,1)S(1)} collective-permute-done((bf16[1,512,8,128]{3,1,2,0:T(8,128)(2,1)}, bf16[1,512,8,128]{3,1,2,0:T(8,128)(2,1)S(1)}, u32[]{:S(2)}, u32[]{:S(2)}) %collective-permute-start.30) | collective-permute-done | bytes 1048608 | tf_op jit(solution)/shard_map/ppermute | solution.py:68
  1356.9 22.8 collective-permute-start.77
  1388.6 31.0 %collective-permute-done.32 = bf16[1,512,8,128]{3,1,2,0:T(8,128)(2,1)} collective-permute-done((bf16[1,512,8,128]{3,1,2,0:T(8,128)(2,1)S(1)}, bf16[1,512,8,128]{3,1,2,0:T(8,128)(2,1)}, u32[]{:S(2)}, u32[]{:S(2)}) %collective-permute-start.32) | collective-permute-done | bytes 1048608 | tf_op jit(solution)/shard_map/ppermute | solution.py:68
  1476.0 30.6 %collective-permute-done.34 = bf16[1,512,8,128]{3,1,2,0:T(8,128)(2,1)S(1)} collective-permute-done((bf16[1,512,8,128]{3,1,2,0:T(8,128)(2,1)}, bf16[1,512,8,128]{3,1,2,0:T(8,128)(2,1)S(1)}, u32[]{:S(2)}, u32[]{:S(2)}) %collective-permute-start.34) | collective-permute-done | bytes 1048608 | tf_op jit(solution)/shard_map/ppermute | solution.py:68
  1560.6 31.0 %collective-permute-done.36 = bf16[1,512,8,128]{3,1,2,0:T(8,128)(2,1)} collective-permute-done((bf16[1,512,8,128]{3,1,2,0:T(8,128)(2,1)S(1)}, bf16[1,512,8,128]{3,1,2,0:T(8,128)(2,1)}, u32[]{:S(2)}, u32[]{:S(2)}) %collective-permute-start.36) | collective-permute-done | bytes 1048608 | tf_op jit(solution)/shard_map/ppermute | solution.py:68
  1647.8 30.6 %collective-permute-done.38 = bf16[1,512,8,128]{3,1,2,0:T(8,128)(2,1)S(1)} collective-permute-done((bf16[1,512,8,128]{3,1,2,0:T(8,128)(2,1)}, bf16[1,512,8,128]{3,1,2,0:T(8,128)(2,1)S(1)}, u32[]{:S(2)}, u32[]{:S(2)}) %collective-permute-start.38) | collective-permute-done | bytes 1048608 | tf_op jit(solution)/shard_map/ppermute | solution.py:68
  1732.7 31.0 %collective-permute-done.40 = bf16[1,512,8,128]{3,1,2,0:T(8,128)(2,1)} collective-permute-done((bf16[1,512,8,128]{3,1,2,0:T(8,128)(2,1)S(1)}, bf16[1,512,8,128]{3,1,2,0:T(8,128)(2,1)}, u32[]{:S(2)}, u32[]{:S(2)}) %collective-permute-start.40) | collective-permute-done | bytes 1048608 | tf_op jit(solution)/shard_map/ppermute | solution.py:68
  1819.8 30.6 %collective-permute-done.42 = bf16[1,512,8,128]{3,1,2,0:T(8,128)(2,1)S(1)} collective-permute-done((bf16[1,512,8,128]{3,1,2,0:T(8,128)(2,1)}, bf16[1,512,8,128]{3,1,2,0:T(8,128)(2,1)S(1)}, u32[]{:S(2)}, u32[]{:S(2)}) %collective-permute-start.42) | collective-permute-done | bytes 1048608 | tf_op jit(solution)/shard_map/ppermute | solution.py:68
  1904.5 31.0 %collective-permute-done.44 = bf16[1,512,8,128]{3,1,2,0:T(8,128)(2,1)} collective-permute-done((bf16[1,512,8,128]{3,1,2,0:T(8,128)(2,1)S(1)}, bf16[1,512,8,128]{3,1,2,0:T(8,128)(2,1)}, u32[]{:S(2)}, u32[]{:S(2)}) %collective-permute-start.44) | collective-permute-done | bytes 1048608 | tf_op jit(solution)/shard_map/ppermute | solution.py:68
  1991.8 30.6 %collective-permute-done.46 = bf16[1,512,8,128]{3,1,2,0:T(8,128)(2,1)S(1)} collective-permute-done((bf16[1,512,8,128]{3,1,2,0:T(8,128)(2,1)}, bf16[1,512,8,128]{3,1,2,0:T(8,128)(2,1)S(1)}, u32[]{:S(2)}, u32[]{:S(2)}) %collective-permute-start.46) | collective-permute-done | bytes 1048608 | tf_op jit(solution)/shard_map/ppermute | solution.py:68
  2076.5 31.0 %collective-permute-done.48 = bf16[1,512,8,128]{3,1,2,0:T(8,128)(2,1)} collective-permute-done((bf16[1,512,8,128]{3,1,2,0:T(8,128)(2,1)S(1)}, bf16[1,512,8,128]{3,1,2,0:T(8,128)(2,1)}, u32[]{:S(2)}, u32[]{:S(2)}) %collective-permute-start.48) | collective-permute-done | bytes 1048608 | tf_op jit(solution)/shard_map/ppermute | solution.py:68
  2163.7 30.6 %collective-permute-done.50 = bf16[1,512,8,128]{3,1,2,0:T(8,128)(2,1)S(1)} collective-permute-done((bf16[1,512,8,128]{3,1,2,0:T(8,128)(2,1)}, bf16[1,512,8,128]{3,1,2,0:T(8,128)(2,1)S(1)}, u32[]{:S(2)}, u32[]{:S(2)}) %collective-permute-start.50) | collective-permute-done | bytes 1048608 | tf_op jit(solution)/shard_map/ppermute | solution.py:68
  2248.6 31.0 %collective-permute-done.52 = bf16[1,512,8,128]{3,1,2,0:T(8,128)(2,1)} collective-permute-done((bf16[1,512,8,128]{3,1,2,0:T(8,128)(2,1)S(1)}, bf16[1,512,8,128]{3,1,2,0:T(8,128)(2,1)}, u32[]{:S(2)}, u32[]{:S(2)}) %collective-permute-start.52) | collective-permute-done | bytes 1048608 | tf_op jit(solution)/shard_map/ppermute | solution.py:68
  2335.8 30.6 %collective-permute-done.54 = bf16[1,512,8,128]{3,1,2,0:T(8,128)(2,1)S(1)} collective-permute-done((bf16[1,512,8,128]{3,1,2,0:T(8,128)(2,1)}, bf16[1,512,8,128]{3,1,2,0:T(8,128)(2,1)S(1)}, u32[]{:S(2)}, u32[]{:S(2)}) %collective-permute-start.54) | collective-permute-done | bytes 1048608 | tf_op jit(solution)/shard_map/ppermute | solution.py:68
  2420.5 31.0 %collective-permute-done.56 = bf16[1,512,8,128]{3,1,2,0:T(8,128)(2,1)} collective-permute-done((bf16[1,512,8,128]{3,1,2,0:T(8,128)(2,1)S(1)}, bf16[1,512,8,128]{3,1,2,0:T(8,128)(2,1)}, u32[]{:S(2)}, u32[]{:S(2)}) %collective-permute-start.56) | collective-permute-done | bytes 1048608 | tf_op jit(solution)/shard_map/ppermute | solution.py:68
  2507.8 30.6 %collective-permute-done.58 = bf16[1,512,8,128]{3,1,2,0:T(8,128)(2,1)} collective-permute-done((bf16[1,512,8,128]{3,1,2,0:T(8,128)(2,1)}, bf16[1,512,8,128]{3,1,2,0:T(8,128)(2,1)}, u32[]{:S(2)}, u32[]{:S(2)}) %collective-permute-start.58) | collective-permute-done | bytes 1048608 | tf_op jit(solution)/shard_map/ppermute | solution.py:68
  2599.7 26.0 collective-permute-done.60
  (748 shorter events, 1900.6 us)
Async XLA Ops:
  144.5 116.5 %collective-permute-start.63 = (f32[1,512,8,128]{3,1,2,0:T(8,128)}, f32[1,512,8,128]{3,1,2,0:T(8,128)}, u32[]{:S(2)}, u32[]{:S(2)}) collective-permute-start(f32[1,512,8,128]{3,1,2,0:T(8,128)} %add.507), channel_id=1, source_target_pairs={{0,1},{1,2},{2,3},{3,4},{4,5},{5,6},{6,7},{7,8},{8,9},{9,10},{10,1... | collective-permute-start | bytes 6291464 | tf_op jit(solution)/shard_map/ppermute | solution.py:68
  351.2 83.7 %collective-permute-start.98 = (f32[1,512,8,128]{3,1,2,0:T(8,128)}, f32[1,512,8,128]{3,1,2,0:T(8,128)}, u32[]{:S(2)}, u32[]{:S(2)}) collective-permute-start(f32[1,512,8,128]{3,1,2,0:T(8,128)} %add.542), channel_id=1, source_target_pairs={{0,1},{1,2},{2,3},{3,4},{4,5},{5,6},{6,7},{7,8},{8,9},{9,10},{10,1... | collective-permute-start | bytes 6291464 | tf_op jit(solution)/shard_map/ppermute | solution.py:68
  438.1 81.8 %collective-permute-start.99 = (f32[1,512,8,128]{3,1,2,0:T(8,128)}, f32[1,512,8,128]{3,1,2,0:T(8,128)}, u32[]{:S(2)}, u32[]{:S(2)}) collective-permute-start(f32[1,512,8,128]{3,1,2,0:T(8,128)} %add.543), channel_id=1, source_target_pairs={{0,1},{1,2},{2,3},{3,4},{4,5},{5,6},{6,7},{7,8},{8,9},{9,10},{10,1... | collective-permute-start | bytes 6291464 | tf_op jit(solution)/shard_map/ppermute | solution.py:68
  523.1 83.6 %collective-permute-start.100 = (f32[1,512,8,128]{3,1,2,0:T(8,128)}, f32[1,512,8,128]{3,1,2,0:T(8,128)}, u32[]{:S(2)}, u32[]{:S(2)}) collective-permute-start(f32[1,512,8,128]{3,1,2,0:T(8,128)} %add.544), channel_id=1, source_target_pairs={{0,1},{1,2},{2,3},{3,4},{4,5},{5,6},{6,7},{7,8},{8,9},{9,10},{10,1... | collective-permute-start | bytes 6291464 | tf_op jit(solution)/shard_map/ppermute | solution.py:68
  610.0 82.1 %collective-permute-start.101 = (f32[1,512,8,128]{3,1,2,0:T(8,128)}, f32[1,512,8,128]{3,1,2,0:T(8,128)}, u32[]{:S(2)}, u32[]{:S(2)}) collective-permute-start(f32[1,512,8,128]{3,1,2,0:T(8,128)} %add.545), channel_id=1, source_target_pairs={{0,1},{1,2},{2,3},{3,4},{4,5},{5,6},{6,7},{7,8},{8,9},{9,10},{10,1... | collective-permute-start | bytes 6291464 | tf_op jit(solution)/shard_map/ppermute | solution.py:68
  695.3 83.5 %collective-permute-start.102 = (f32[1,512,8,128]{3,1,2,0:T(8,128)}, f32[1,512,8,128]{3,1,2,0:T(8,128)}, u32[]{:S(2)}, u32[]{:S(2)}) collective-permute-start(f32[1,512,8,128]{3,1,2,0:T(8,128)} %add.546), channel_id=1, source_target_pairs={{0,1},{1,2},{2,3},{3,4},{4,5},{5,6},{6,7},{7,8},{8,9},{9,10},{10,1... | collective-permute-start | bytes 6291464 | tf_op jit(solution)/shard_map/ppermute | solution.py:68
  867.1 83.7 %collective-permute-start.104 = (f32[1,512,8,128]{3,1,2,0:T(8,128)}, f32[1,512,8,128]{3,1,2,0:T(8,128)}, u32[]{:S(2)}, u32[]{:S(2)}) collective-permute-start(f32[1,512,8,128]{3,1,2,0:T(8,128)} %add.548), channel_id=1, source_target_pairs={{0,1},{1,2},{2,3},{3,4},{4,5},{5,6},{6,7},{7,8},{8,9},{9,10},{10,1... | collective-permute-start | bytes 6291464 | tf_op jit(solution)/shard_map/ppermute | solution.py:68
  1013.1 81.9 %collective-permute-start.73 = (f32[1,512,8,128]{3,1,2,0:T(8,128)}, f32[1,512,8,128]{3,1,2,0:T(8,128)}, u32[]{:S(2)}, u32[]{:S(2)}) collective-permute-start(f32[1,512,8,128]{3,1,2,0:T(8,128)} %add.517), channel_id=1, source_target_pairs={{0,1},{1,2},{2,3},{3,4},{4,5},{5,6},{6,7},{7,8},{8,9},{9,10},{10,1... | collective-permute-start | bytes 6291464 | tf_op jit(solution)/shard_map/ppermute | solution.py:68
  1039.1 83.5 %collective-permute-start.106 = (f32[1,512,8,128]{3,1,2,0:T(8,128)}, f32[1,512,8,128]{3,1,2,0:T(8,128)}, u32[]{:S(2)}, u32[]{:S(2)}) collective-permute-start(f32[1,512,8,128]{3,1,2,0:T(8,128)} %add.550), channel_id=1, source_target_pairs={{0,1},{1,2},{2,3},{3,4},{4,5},{5,6},{6,7},{7,8},{8,9},{9,10},{10,1... | collective-permute-start | bytes 6291464 | tf_op jit(solution)/shard_map/ppermute | solution.py:68
  1125.8 82.0 %collective-permute-start.107 = (f32[1,512,8,128]{3,1,2,0:T(8,128)}, f32[1,512,8,128]{3,1,2,0:T(8,128)}, u32[]{:S(2)}, u32[]{:S(2)}) collective-permute-start(f32[1,512,8,128]{3,1,2,0:T(8,128)} %add.551), channel_id=1, source_target_pairs={{0,1},{1,2},{2,3},{3,4},{4,5},{5,6},{6,7},{7,8},{8,9},{9,10},{10,1... | collective-permute-start | bytes 6291464 | tf_op jit(solution)/shard_map/ppermute | solution.py:68
  1185.1 81.9 %collective-permute-start.75 = (f32[1,512,8,128]{3,1,2,0:T(8,128)}, f32[1,512,8,128]{3,1,2,0:T(8,128)}, u32[]{:S(2)}, u32[]{:S(2)}) collective-permute-start(f32[1,512,8,128]{3,1,2,0:T(8,128)} %add.519), channel_id=1, source_target_pairs={{0,1},{1,2},{2,3},{3,4},{4,5},{5,6},{6,7},{7,8},{8,9},{9,10},{10,1... | collective-permute-start | bytes 6291464 | tf_op jit(solution)/shard_map/ppermute | solution.py:68
  1211.1 83.5 %collective-permute-start.108 = (f32[1,512,8,128]{3,1,2,0:T(8,128)}, f32[1,512,8,128]{3,1,2,0:T(8,128)}, u32[]{:S(2)}, u32[]{:S(2)}) collective-permute-start(f32[1,512,8,128]{3,1,2,0:T(8,128)} %add.552), channel_id=1, source_target_pairs={{0,1},{1,2},{2,3},{3,4},{4,5},{5,6},{6,7},{7,8},{8,9},{9,10},{10,1... | collective-permute-start | bytes 6291464 | tf_op jit(solution)/shard_map/ppermute | solution.py:68
  1297.8 81.8 %collective-permute-start.109 = (f32[1,512,8,128]{3,1,2,0:T(8,128)}, f32[1,512,8,128]{3,1,2,0:T(8,128)}, u32[]{:S(2)}, u32[]{:S(2)}) collective-permute-start(f32[1,512,8,128]{3,1,2,0:T(8,128)} %add.553), channel_id=1, source_target_pairs={{0,1},{1,2},{2,3},{3,4},{4,5},{5,6},{6,7},{7,8},{8,9},{9,10},{10,1... | collective-permute-start | bytes 6291464 | tf_op jit(solution)/shard_map/ppermute | solution.py:68
  1356.9 82.1 %collective-permute-start.77 = (f32[1,512,8,128]{3,1,2,0:T(8,128)}, f32[1,512,8,128]{3,1,2,0:T(8,128)}, u32[]{:S(2)}, u32[]{:S(2)}) collective-permute-start(f32[1,512,8,128]{3,1,2,0:T(8,128)} %add.521), channel_id=1, source_target_pairs={{0,1},{1,2},{2,3},{3,4},{4,5},{5,6},{6,7},{7,8},{8,9},{9,10},{10,1... | collective-permute-start | bytes 6291464 | tf_op jit(solution)/shard_map/ppermute | solution.py:68
  1382.9 83.8 %collective-permute-start.110 = (f32[1,512,8,128]{3,1,2,0:T(8,128)}, f32[1,512,8,128]{3,1,2,0:T(8,128)}, u32[]{:S(2)}, u32[]{:S(2)}) collective-permute-start(f32[1,512,8,128]{3,1,2,0:T(8,128)} %add.554), channel_id=1, source_target_pairs={{0,1},{1,2},{2,3},{3,4},{4,5},{5,6},{6,7},{7,8},{8,9},{9,10},{10,1... | collective-permute-start | bytes 6291464 | tf_op jit(solution)/shard_map/ppermute | solution.py:68
  1528.9 81.9 %collective-permute-start.79 = (f32[1,512,8,128]{3,1,2,0:T(8,128)}, f32[1,512,8,128]{3,1,2,0:T(8,128)}, u32[]{:S(2)}, u32[]{:S(2)}) collective-permute-start(f32[1,512,8,128]{3,1,2,0:T(8,128)} %add.523), channel_id=1, source_target_pairs={{0,1},{1,2},{2,3},{3,4},{4,5},{5,6},{6,7},{7,8},{8,9},{9,10},{10,1... | collective-permute-start | bytes 6291464 | tf_op jit(solution)/shard_map/ppermute | solution.py:68
  1554.9 83.5 %collective-permute-start.112 = (f32[1,512,8,128]{3,1,2,0:T(8,128)}, f32[1,512,8,128]{3,1,2,0:T(8,128)}, u32[]{:S(2)}, u32[]{:S(2)}) collective-permute-start(f32[1,512,8,128]{3,1,2,0:T(8,128)} %add.556), channel_id=1, source_target_pairs={{0,1},{1,2},{2,3},{3,4},{4,5},{5,6},{6,7},{7,8},{8,9},{9,10},{10,1... | collective-permute-start | bytes 6291464 | tf_op jit(solution)/shard_map/ppermute | solution.py:68
  1641.8 82.0 %collective-permute-start.113 = (f32[1,512,8,128]{3,1,2,0:T(8,128)}, f32[1,512,8,128]{3,1,2,0:T(8,128)}, u32[]{:S(2)}, u32[]{:S(2)}) collective-permute-start(f32[1,512,8,128]{3,1,2,0:T(8,128)} %add.557), channel_id=1, source_target_pairs={{0,1},{1,2},{2,3},{3,4},{4,5},{5,6},{6,7},{7,8},{8,9},{9,10},{10,1... | collective-permute-start | bytes 6291464 | tf_op jit(solution)/shard_map/ppermute | solution.py:68
  1701.0 81.9 %collective-permute-start.81 = (f32[1,512,8,128]{3,1,2,0:T(8,128)}, f32[1,512,8,128]{3,1,2,0:T(8,128)}, u32[]{:S(2)}, u32[]{:S(2)}) collective-permute-start(f32[1,512,8,128]{3,1,2,0:T(8,128)} %add.525), channel_id=1, source_target_pairs={{0,1},{1,2},{2,3},{3,4},{4,5},{5,6},{6,7},{7,8},{8,9},{9,10},{10,1... | collective-permute-start | bytes 6291464 | tf_op jit(solution)/shard_map/ppermute | solution.py:68
  1727.0 83.4 %collective-permute-start.114 = (f32[1,512,8,128]{3,1,2,0:T(8,128)}, f32[1,512,8,128]{3,1,2,0:T(8,128)}, u32[]{:S(2)}, u32[]{:S(2)}) collective-permute-start(f32[1,512,8,128]{3,1,2,0:T(8,128)} %add.558), channel_id=1, source_target_pairs={{0,1},{1,2},{2,3},{3,4},{4,5},{5,6},{6,7},{7,8},{8,9},{9,10},{10,1... | collective-permute-start | bytes 6291464 | tf_op jit(solution)/shard_map/ppermute | solution.py:68
  1872.7 82.1 %collective-permute-start.83 = (f32[1,512,8,128]{3,1,2,0:T(8,128)}, f32[1,512,8,128]{3,1,2,0:T(8,128)}, u32[]{:S(2)}, u32[]{:S(2)}) collective-permute-start(f32[1,512,8,128]{3,1,2,0:T(8,128)} %add.527), channel_id=1, source_target_pairs={{0,1},{1,2},{2,3},{3,4},{4,5},{5,6},{6,7},{7,8},{8,9},{9,10},{10,1... | collective-permute-start | bytes 6291464 | tf_op jit(solution)/shard_map/ppermute | solution.py:68
  1898.7 83.7 %collective-permute-start.116 = (f32[1,512,8,128]{3,1,2,0:T(8,128)}, f32[1,512,8,128]{3,1,2,0:T(8,128)}, u32[]{:S(2)}, u32[]{:S(2)}) collective-permute-start(f32[1,512,8,128]{3,1,2,0:T(8,128)} %add.560), channel_id=1, source_target_pairs={{0,1},{1,2},{2,3},{3,4},{4,5},{5,6},{6,7},{7,8},{8,9},{9,10},{10,1... | collective-permute-start | bytes 6291464 | tf_op jit(solution)/shard_map/ppermute | solution.py:68
  2044.7 81.9 %collective-permute-start.85 = (f32[1,512,8,128]{3,1,2,0:T(8,128)}, f32[1,512,8,128]{3,1,2,0:T(8,128)}, u32[]{:S(2)}, u32[]{:S(2)}) collective-permute-start(f32[1,512,8,128]{3,1,2,0:T(8,128)} %add.529), channel_id=1, source_target_pairs={{0,1},{1,2},{2,3},{3,4},{4,5},{5,6},{6,7},{7,8},{8,9},{9,10},{10,1... | collective-permute-start | bytes 6291464 | tf_op jit(solution)/shard_map/ppermute | solution.py:68
  2070.8 83.5 %collective-permute-start.118 = (f32[1,512,8,128]{3,1,2,0:T(8,128)}, f32[1,512,8,128]{3,1,2,0:T(8,128)}, u32[]{:S(2)}, u32[]{:S(2)}) collective-permute-start(f32[1,512,8,128]{3,1,2,0:T(8,128)} %add.562), channel_id=1, source_target_pairs={{0,1},{1,2},{2,3},{3,4},{4,5},{5,6},{6,7},{7,8},{8,9},{9,10},{10,1... | collective-permute-start | bytes 6291464 | tf_op jit(solution)/shard_map/ppermute | solution.py:68
  2157.6 82.0 %collective-permute-start.119 = (f32[1,512,8,128]{3,1,2,0:T(8,128)}, f32[1,512,8,128]{3,1,2,0:T(8,128)}, u32[]{:S(2)}, u32[]{:S(2)}) collective-permute-start(f32[1,512,8,128]{3,1,2,0:T(8,128)} %add.563), channel_id=1, source_target_pairs={{0,1},{1,2},{2,3},{3,4},{4,5},{5,6},{6,7},{7,8},{8,9},{9,10},{10,1... | collective-permute-start | bytes 6291464 | tf_op jit(solution)/shard_map/ppermute | solution.py:68
  2216.9 81.9 %collective-permute-start.87 = (f32[1,512,8,128]{3,1,2,0:T(8,128)}, f32[1,512,8,128]{3,1,2,0:T(8,128)}, u32[]{:S(2)}, u32[]{:S(2)}) collective-permute-start(f32[1,512,8,128]{3,1,2,0:T(8,128)} %add.531), channel_id=1, source_target_pairs={{0,1},{1,2},{2,3},{3,4},{4,5},{5,6},{6,7},{7,8},{8,9},{9,10},{10,1... | collective-permute-start | bytes 6291464 | tf_op jit(solution)/shard_map/ppermute | solution.py:68
  2242.9 83.5 %collective-permute-start.120 = (f32[1,512,8,128]{3,1,2,0:T(8,128)}, f32[1,512,8,128]{3,1,2,0:T(8,128)}, u32[]{:S(2)}, u32[]{:S(2)}) collective-permute-start(f32[1,512,8,128]{3,1,2,0:T(8,128)} %add.564), channel_id=1, source_target_pairs={{0,1},{1,2},{2,3},{3,4},{4,5},{5,6},{6,7},{7,8},{8,9},{9,10},{10,1... | collective-permute-start | bytes 6291464 | tf_op jit(solution)/shard_map/ppermute | solution.py:68
  2388.8 82.1 %collective-permute-start.89 = (f32[1,512,8,128]{3,1,2,0:T(8,128)}, f32[1,512,8,128]{3,1,2,0:T(8,128)}, u32[]{:S(2)}, u32[]{:S(2)}) collective-permute-start(f32[1,512,8,128]{3,1,2,0:T(8,128)} %add.533), channel_id=1, source_target_pairs={{0,1},{1,2},{2,3},{3,4},{4,5},{5,6},{6,7},{7,8},{8,9},{9,10},{10,1... | collective-permute-start | bytes 6291464 | tf_op jit(solution)/shard_map/ppermute | solution.py:68
  2414.8 83.6 %collective-permute-start.122 = (f32[1,512,8,128]{3,1,2,0:T(8,128)}, f32[1,512,8,128]{3,1,2,0:T(8,128)}, u32[]{:S(2)}, u32[]{:S(2)}) collective-permute-start(f32[1,512,8,128]{3,1,2,0:T(8,128)} %add.566), channel_id=1, source_target_pairs={{0,1},{1,2},{2,3},{3,4},{4,5},{5,6},{6,7},{7,8},{8,9},{9,10},{10,1... | collective-permute-start | bytes 6291464 | tf_op jit(solution)/shard_map/ppermute | solution.py:68
  2501.7 83.7 %collective-permute-start.123 = (f32[1,512,8,128]{3,1,2,0:T(8,128)}, f32[1,512,8,128]{3,1,2,0:T(8,128)}, u32[]{:S(2)}, u32[]{:S(2)}) collective-permute-start(f32[1,512,8,128]{3,1,2,0:T(8,128)} %add.567), channel_id=1, source_target_pairs={{0,1},{1,2},{2,3},{3,4},{4,5},{5,6},{6,7},{7,8},{8,9},{9,10},{10,1... | collective-permute-start | bytes 6291464 | tf_op jit(solution)/shard_map/ppermute | solution.py:68
  2562.8 82.3 %collective-permute-start.91 = (f32[1,512,8,128]{3,1,2,0:T(8,128)}, f32[1,512,8,128]{3,1,2,0:T(8,128)}, u32[]{:S(2)}, u32[]{:S(2)}) collective-permute-start(f32[1,512,8,128]{3,1,2,0:T(8,128)} %add.535), channel_id=1, source_target_pairs={{0,1},{1,2},{2,3},{3,4},{4,5},{5,6},{6,7},{7,8},{8,9},{9,10},{10,1... | collective-permute-start | bytes 6291464 | tf_op jit(solution)/shard_map/ppermute | solution.py:68
  2588.9 83.8 %collective-permute-start.124 = (f32[1,512,8,128]{3,1,2,0:T(8,128)}, f32[1,512,8,128]{3,1,2,0:T(8,128)}, u32[]{:S(2)}, u32[]{:S(2)}) collective-permute-start(f32[1,512,8,128]{3,1,2,0:T(8,128)} %add.568), channel_id=1, source_target_pairs={{0,1},{1,2},{2,3},{3,4},{4,5},{5,6},{6,7},{7,8},{8,9},{9,10},{10,1... | collective-permute-start | bytes 6291464 | tf_op jit(solution)/shard_map/ppermute | solution.py:68
  (186 other events, 5549.4 us)
where the time goes:
time: 2770 us; the launch traced here: 2760 us
  waiting for transfers between devices  1470 us (53%)
  starting transfers between devices  748 us (27%)
  other arithmetic  283 us (10%)
  matrix products  213 us (8%)
  local copies, waits for them, and re-layouts  34.2 us (1%)
    ppermute x124, waiting for transfers between devices, body(): k, v, dk, dv = [lax.ppermute(x, 'cp', perm) for x in (k, v, dk, dv)]  1380 us
    ppermute x124, starting transfers between devices, body(): k, v, dk, dv = [lax.ppermute(x, 'cp', perm) for x in (k, v, dk, dv)]  711 us
    add x62, other arithmetic, body(): dq, dk, dv = (dq + ddq, dk + ddk, dv + ddv)  263 us
    dot_general x33, matrix products, _block(): jnp.einsum('bqhgd,bkhd->bhgqk', do, v, preferred_element_type=jnp.float32)  68.1 us
  transfers between devices with their start and end apart: 134, of which 71 were waited for; matrix products, arithmetic and copies ran while one was open for 19% of the time, Pallas kernels for 0%

commit v1 on v0

v1 whole, which is shorter than its diff:
```python
import functools

import jax
import jax.numpy as jnp
from jax import lax
from jax.experimental import pallas as pl
from jax.experimental.pallas import tpu as pltpu
from jax.sharding import Mesh, PartitionSpec as P

LOG2E = 1.4426950408889634
BT = 512


def _attn_kernel(scale, n, info, q, do, qt, dot, k, kt, vt, lse, dlt, dq, dkt, dvt, p_s, ds_s, lse_b, dlt_b):
    core, half = info[0], info[1]
    f32, bf16 = jnp.float32, jnp.bfloat16
    dkt[...] = jnp.zeros_like(dkt)
    dvt[...] = jnp.zeros_like(dvt)
    dq[...] = jnp.zeros_like(dq)

    def rows(i):
        return pl.ds(pl.multiple_of(i * BT, BT), BT)

    def stage1(qb, kb, slot, diag):
        qs, ks = rows(qb), rows(kb)
        s = jnp.dot(q[qs, :], kt[:, ks], preferred_element_type=f32)
        dp = jnp.dot(do[qs, :], vt[:, ks], preferred_element_type=f32)
        lb = jnp.tile(lse_b[...], (1, BT // 128))
        db = jnp.tile(dlt_b[...], (1, BT // 128))
        p = jnp.exp2(s * (scale * LOG2E) - lb)
        if diag:
            hi = (2 * qb >= n).astype(jnp.int32)
            r = lax.broadcasted_iota(jnp.int32, (BT, BT), 0)
            c = lax.broadcasted_iota(jnp.int32, (BT, BT), 1)
            e = jnp.where(hi == 1, 1 - core, core)
            qp = (r // 256 * 2 + e) * 256 + r % 256
            jj = c // 128 % 2
            kp = (c // 256 * 2 + jnp.where(hi == 1, 1 - jj, jj)) * 256 + half * 128 + c % 128
            p = jnp.where(kp <= qp, p, 0.0)
        p_s[slot] = p.astype(bf16)
        ds_s[slot] = (p * (dp - db)).astype(bf16)

    def stage2(qb, kb, slot):
        qs, ks = rows(qb), rows(kb)
        dvt[:, ks] += jnp.dot(dot[:, qs], p_s[slot], preferred_element_type=f32)
        dkt[:, ks] += jnp.dot(qt[:, qs], ds_s[slot], preferred_element_type=f32)
        dq[qs, :] += jnp.dot(ds_s[slot], k[ks, :], preferred_element_type=f32)

    def stats(qb):
        qs = rows(qb)
        lse_b[...] = jnp.broadcast_to(lse[:, qs] * LOG2E, (128, BT)).T
        dlt_b[...] = jnp.broadcast_to(dlt[:, qs], (128, BT)).T

    def row(qb, carry):
        stats(qb)

        def full(kb, carry):
            pq, pk, slot = carry
            stage2(pq, pk, 1 - slot)
            stage1(qb, kb, slot, False)
            return qb, kb, 1 - slot

        pq, pk, slot = lax.fori_loop(0, qb, full, carry)
        stage2(pq, pk, 1 - slot)
        stage1(qb, qb, slot, True)
        return qb, qb, 1 - slot

    p_s[1] = jnp.zeros((BT, BT), bf16)
    ds_s[1] = jnp.zeros((BT, BT), bf16)
    pq, pk, slot = lax.fori_loop(0, n, row, (0, 0, 0))
    stage2(pq, pk, 1 - slot)


def _attention(q, do, k, v, lse, dlt, core, half, scale):
    t, d = q.shape
    info = jnp.stack([core, half]).astype(jnp.int32)
    f32 = jnp.float32
    vm = pl.BlockSpec(memory_space=pltpu.VMEM)
    return pl.pallas_call(
        functools.partial(_attn_kernel, scale, t // BT),
        out_shape=(jax.ShapeDtypeStruct((t, d), f32), jax.ShapeDtypeStruct((d, t), f32), jax.ShapeDtypeStruct((d, t), f32)),
        in_specs=[pl.BlockSpec(memory_space=pltpu.SMEM)] + [vm] * 9,
        out_specs=(vm, vm, vm),
        scratch_shapes=[
            pltpu.VMEM((2, BT, BT), jnp.bfloat16),
            pltpu.VMEM((2, BT, BT), jnp.bfloat16),
            pltpu.VMEM((BT, 128), f32),
            pltpu.VMEM((BT, 128), f32),
        ],
        compiler_params=pltpu.CompilerParams(vmem_limit_bytes=62 * 1024 * 1024),
        cost_estimate=pl.CostEstimate(flops=5 * t * t * d, bytes_accessed=26 * t * d, transcendentals=t * t // 2),
        name='attn_bwd',
    )(info, q, do, q.T, do.T, k, k.T, v.T, lse, dlt)


def solution(mesh):
    x, cp = mesh.devices.shape
    fine = Mesh(mesh.devices.reshape(2, 2, 4, 4, 2), ('xa', 'xb', 'z', 'y', 'core'))
    rows = ('z', 'y', 'core', 'xa', 'xb')
    seq = P(None, rows, None, None)
    stat = P(None, None, rows)
    heads = ('z', 'y', 'xa')

    def body(q, k, v, o, do, lse):
        _, r, h, d = q.shape
        f32 = jnp.float32
        scale = d ** -0.5
        core, half = lax.axis_index('core'), lax.axis_index('xb')
        dlt = jnp.sum(do.astype(f32) * o.astype(f32), axis=-1)[0].T
        st = jnp.stack([lse[0], dlt], axis=1)
        kv = jnp.stack([k[0], v[0]]).transpose(2, 0, 1, 3)
        qd = jnp.stack([q[0], do[0]]).transpose(2, 0, 1, 3)
        kv, qd, st = [lax.all_to_all(a, heads, 0, 0, tiled=True) for a in (kv, qd, st)]

        def order(a):
            a = a.reshape(16, 2, *a.shape[1:])
            return jnp.concatenate([a[:, 0], a[::-1, 1]], axis=0)

        kv, qd, st = order(kv), order(qd), order(st)
        kv = lax.all_gather(kv, 'core', axis=2)
        qd = lax.all_gather(qd, 'xb', axis=2)
        st = lax.all_gather(st, 'xb', axis=2)
        t = 64 * r
        kk, vv = [kv[:, i].reshape(t, d) for i in range(2)]
        qq, dd = [qd[:, i].reshape(t, d) for i in range(2)]
        ll, dl = [st[:, i].reshape(1, t) for i in range(2)]
        dq, dkt, dvt = _attention(qq, dd, kk, vv, ll, dl, core, half, scale)

        def swap(a, axis):
            i = lax.axis_index(axis)
            mine = lax.dynamic_index_in_dim(a, i, 1, keepdims=False)
            other = lax.dynamic_index_in_dim(a, 1 - i, 1, keepdims=False)
            return mine + lax.ppermute(other, axis, [(0, 1), (1, 0)])

        dq = swap(dq.reshape(32, 2, r, d), 'xb')
        dk = swap(dkt.T.reshape(32, 2, r, d), 'core')
        dv = swap(dvt.T.reshape(32, 2, r, d), 'core')
        out = jnp.stack([dq * scale, dk * scale, dv], axis=1).astype(jnp.bfloat16)
        out = jnp.stack([out[:16], out[16:][::-1]], axis=1).reshape(32, 3, r, d)
        out = lax.all_to_all(out, heads, 0, 0, tiled=True)
        out = out.transpose(1, 2, 0, 3)
        return out[0][None], out[1][None], out[2][None]

    return jax.shard_map(body, mesh=fine, in_specs=(seq, seq, seq, seq, seq, stat), out_specs=(seq, seq, seq), check_vma=False)
```

time: 2770 us -> 444 us (0.16)
  waiting for transfers between devices: 1470 us -> 68 us
  starting transfers between devices: 748 us -> 12.1 us
  other arithmetic: 283 us -> 12.1 us
  matrix products: 213 us -> 0 us
  blocking collectives: 0 us -> 132 us
  Pallas kernels: 0 us -> 114 us
  local copies, waits for them, and re-layouts: 34.2 us -> 87.2 us
    ppermute x126 -> x3, waiting for transfers between devices: 1380 us -> 32.6 us  [swap(): return mine + lax.ppermute(other, axis, [(0, 1), (1, 0)])]
    ppermute x126 -> x3, starting transfers between devices: 717 us -> 1.07 us  [swap(): return mine + lax.ppermute(other, axis, [(0, 1), (1, 0)])]
    add x62 -> x0, other arithmetic: 263 us -> none  [body(): dq, dk, dv = (dq + ddq, dk + ddk, dv + ddv)]
    dot_general x165 -> x0, matrix products: 213 us -> none  [the longest x33 68.1 us: _block(): jnp.einsum('bqhgd,bkhd->bhgqk', do, v, preferred_element_type=jnp.float32)]
    all_to_all x0 -> x3, blocking collectives: none -> 126 us  [the longest x2 75.6 us: body(): lax.all_to_all(a, heads, 0, 0, tiled=True)]
    pallas_call x0 -> x1, Pallas kernels: none -> 114 us  [_attention(): pl.pallas_call(functools.partial(_attn_kernel, scale, t // BT), out_shape...]
    all_to_all x8 -> x1, waiting for transfers between devices: 85.8 us -> 5.56 us  [body(): lax.all_to_all(a, heads, 0, 0, tiled=True)]
    all_gather x0 -> x2, waiting for transfers between devices: none -> 29.9 us  [the longest x1 29.9 us: body(): qd = lax.all_gather(qd, 'xb', axis=2)]
  transfers between devices with their start and end apart: 134 -> 6, of which waited for: 71 -> 3; matrix products, arithmetic and copies ran while one was open for 19% -> 8% of each run, Pallas kernels for 0% -> 0%
where the time goes in v1:
time: 444 us; the launch traced here: 440 us
  blocking collectives  132 us (30%)
  Pallas kernels  114 us (26%)
  local copies, waits for them, and re-layouts  87.2 us (20%)
  waiting for transfers between devices  68 us (15%)
  between operations  14.3 us (3%)
  starting transfers between devices  12.1 us (3%)
  other arithmetic  12.1 us (3%)
    pallas_call x1, Pallas kernels, _attention(): pl.pallas_call(functools.partial(_attn_kernel, scale, t // BT), out_shape...  114 us
    all_to_all x2, blocking collectives, body(): lax.all_to_all(a, heads, 0, 0, tiled=True)  75.6 us
    all_to_all x1, blocking collectives, body(): out = lax.all_to_all(out, heads, 0, 0, tiled=True)  50.8 us
    ppermute x3, waiting for transfers between devices, swap(): return mine + lax.ppermute(other, axis, [(0, 1), (1, 0)])  32.6 us
    unnamed x30, local copies, waits for them, and re-layouts  31.3 us
    all_gather x1, waiting for transfers between devices, body(): qd = lax.all_gather(qd, 'xb', axis=2)  29.9 us
    dynamic_slice x1, local copies, waits for them, and re-layouts, swap(): mine = lax.dynamic_index_in_dim(a, i, 1, keepdims=False)  13.9 us
    all_to_all x1, starting transfers between devices, body(): lax.all_to_all(a, heads, 0, 0, tiled=True)  11 us
  transfers between devices with their start and end apart: 6, of which 3 were waited for; matrix products, arithmetic and copies ran while one was open for 8% of the time, Pallas kernels for 0%

profile of v1, /device:TPU:120, one launch (start us, length us, event | category | flops | bytes accessed | tf_op | source)
XLA Modules:
  0.0 439.6 jit_solution(10536109097881114577)
XLA Ops:
  7.2 1.7 copy.116
  9.6 38.5 %all_to_all.20 = bf16[32,2,128,128]{3,2,1,0:T(8,128)(2,1)S(1)} all-to-all(bf16[32,2,128,128]{3,2,1,0:T(8,128)(2,1)S(1)} %maximum_bitcast_fusion.1), channel_id=1, replica_groups=mesh['xa'=2,'xb'=2,'z'=4,'y'=4,'core'=2] {'z','y','xa'}, dimensions={0} | all-to-all | bytes 4194304 | tf_op jit(solution)/shard_map/all_to_all | solution.py:113
  48.3 1.6 pad_maximum_fusion.3
  52.1 37.1 %all_to_all.21 = bf16[32,2,128,128]{3,2,1,0:T(8,128)(2,1)S(1)} all-to-all(bf16[32,2,128,128]{3,2,1,0:T(8,128)(2,1)S(1)} %maximum_bitcast_fusion), channel_id=1, replica_groups=mesh['xa'=2,'xb'=2,'z'=4,'y'=4,'core'=2] {'z','y','xa'}, dimensions={0} | all-to-all | bytes 4194304 | tf_op jit(solution)/shard_map/all_to_all | solution.py:113
  89.5 1.5 pad_maximum_fusion.2
  93.6 11.0 %all-to-all-start.2 = ((f32[32,2,128]{2,1,0:T(2,128)}), f32[32,2,128]{2,1,0:T(2,128)S(1)}, u32[]{:S(2)}, u32[]{:S(2)}) async-start(f32[32,2,128]{2,1,0:T(2,128)} %copy.121), calls=%async_computation.2 | async-start | bytes 65536 | tf_op jit(solution)/shard_map/all_to_all | solution.py:113
  105.2 5.6 %all-to-all-done.2 = f32[32,2,128]{2,1,0:T(2,128)S(1)} async-done(((f32[32,2,128]{2,1,0:T(2,128)}), f32[32,2,128]{2,1,0:T(2,128)S(1)}, u32[]{:S(2)}, u32[]{:S(2)}) %all-to-all-start.2) | async-done | bytes 32800 | tf_op jit(solution)/shard_map/all_to_all | solution.py:113
  110.8 5.5 %all-gather.2 = f32[32,2,256]{2,1,0:T(2,128)S(1)} all-gather(f32[32,2,128]{2,1,0:T(2,128)S(1)} %pad_maximum_fusion.5), channel_id=4, replica_groups=mesh['xa'=2,'xb'=2,'z'=4,'y'=4,'core'=2] {'xb'}, dimensions={2}, use_global_device_ids=true | all-gather | bytes 98304 | tf_op jit(solution)/shard_map/all_gather | solution.py:122
  117.0 4.1 fusion.8
  121.1 2.9 copy.156
  124.0 29.9 %all-gather.6.cloned.1.call-done = bf16[32,2,256,128]{3,2,1,0:T(8,128)(2,1)} async-done(((bf16[32,2,128,128]{3,2,1,0:T(8,128)(2,1)}), bf16[32,2,256,128]{3,2,1,0:T(8,128)(2,1)}) %all-gather.6.cloned.1.call-update) | async-done | bytes 4194320 | tf_op jit(solution)/shard_map/all_gather | solution.py:121
  153.9 4.0 fusion.9
  157.9 4.4 %copy.154 = bf16[8192,128]{0,1:T(8,128)(2,1)} copy(bf16[8192,128]{1,0:T(8,128)(2,1)} %bitcast.100) | data formatting | bytes 4194304 | tf_op jit(solution)/shard_map/reshape;squeeze | solution.py:125
  162.3 2.9 copy.155
  165.2 4.1 copy.157
  169.4 114.1 %attn_bwd.1 = (f32[8192,128]{1,0:T(8,128)}, f32[128,8192]{1,0:T(8,128)}, f32[128,8192]{1,0:T(8,128)}) custom-call(s32[2]{0:T(128)} %pad_add_fusion.info, bf16[8192,128]{1,0:T(8,128)(2,1)} %bitcast.101, bf16[8192,128]{1,0:T(8,128)(2,1)} %bitcast.99, bf16[128,8192]{1,0:T(8,128)(2,1)} %bitcast.112, bf16[128,8192]{1,0:T(8,128)(2,1)} %bitcast.113, ...), custom_call_target="tpu_custom_call" | custom-call | flops 42949672960 | bytes 27262976 | tf_op jit(solution)/shard_map/attn_bwd/pallas_call | solution.py:79
  283.4 6.6 %reshape.33 = f32[32,2,128,128]{2,1,0,3:T(2,128)} reshape(f32[8192,128]{0,1:T(8,128)} %bitcast.108) | data formatting | bytes 8388608 | tf_op jit(solution)/shard_map/reshape | solution.py:136
  290.0 6.6 %reshape.34 = f32[32,2,128,128]{2,1,0,3:T(2,128)} reshape(f32[8192,128]{0,1:T(8,128)} %bitcast.107) | data formatting | bytes 8388608 | tf_op jit(solution)/shard_map/reshape | solution.py:137
  296.6 13.9 %constant_dynamic-slice_fusion.1 = (f32[32,1,128,128]{2,1,0,3:T(1,128)S(1)}, f32[32,1,128,128]{2,1,0,3:T(1,128)}, f32[32,1,128,128]{2,1,0,3:T(1,128)}, f32[32,1,128,128]{2,1,0,3:T(1,128)}) fusion(f32[32,2,128,128]{2,1,0,3:T(2,128)} %reshape.34, s32[]{:T(128)S(6)} %select_n.17, s32[]{:T(128)S(6)} %select_n.18, f32[32,2,128,128]{2,1,0,3:T(2,128)} %reshape.33), kind=kLoop, calls=%fused_computation.30 | loop fusion | bytes 16777224 | tf_op jit(solution)/shard_map/jit(dynamic_index_in_dim)/dynamic_slice | solution.py:131
  310.5 5.7 %copy.151 = f32[32,1,128,128]{3,2,0,1:T(8,128)} copy(f32[32,1,128,128]{2,1,0,3:T(1,128)} %get-tuple-element.42) | data formatting | bytes 4194304
  316.2 5.7 %copy.153 = f32[32,1,128,128]{3,2,0,1:T(8,128)} copy(f32[32,1,128,128]{2,1,0,3:T(1,128)} %get-tuple-element.24) | data formatting | bytes 4194304
  322.4 3.1 dynamic-slice_bitcast_fusion
  326.1 5.7 %copy.150 = f32[32,1,128,128]{3,2,0,1:T(8,128)} copy(f32[32,1,128,128]{2,1,0,3:T(1,128)} %get-tuple-element.43) | data formatting | bytes 4194304
  331.8 3.8 copy.152
  335.6 2.7 fusion.5
  338.5 2.0 fusion.6
  340.5 32.6 %collective-permute-done = f32[32,128,128]{2,1,0:T(8,128)} collective-permute-done((f32[32,128,128]{2,1,0:T(8,128)}, f32[32,128,128]{2,1,0:T(8,128)}, u32[]{:S(2)}, u32[]{:S(2)}) %collective-permute-start) | collective-permute-done | bytes 2097184 | tf_op jit(solution)/shard_map/ppermute | solution.py:133
  373.1 1.9 fusion.7
  376.7 50.8 %all_to_all.22 = bf16[32,3,128,128]{3,2,1,0:T(8,128)(2,1)S(1)} all-to-all(bf16[32,3,128,128]{3,2,1,0:T(8,128)(2,1)S(1)} %bitcast.93), channel_id=1, replica_groups=mesh['xa'=2,'xb'=2,'z'=4,'y'=4,'core'=2] {'z','y','xa'}, dimensions={0} | all-to-all | bytes 6291456 | tf_op jit(solution)/shard_map/all_to_all | solution.py:140
  427.9 1.7 copy.136
  429.5 1.6 copy.137
  431.2 1.6 copy.138
  (53 shorter events, 10.5 us)
Async XLA Ops:
  7.2 1.8 copy-start.5
  7.2 109.8 %all-gather.8.cloned.1.call-start = ((), (), s32[]{:S(2)}) async-start(), calls=%async_computation.5 | async-start | bytes 6291456 | tf_op jit(solution)/shard_map/all_gather | solution.py:120
  49.9 1.2 copy-start.6
  49.9 1.6 copy-start.4
  49.9 104.0 %all-gather.6.cloned.1.call-start = ((), (), s32[]{:S(2)}) async-start(), calls=%async_computation.4 | async-start | bytes 6291456 | tf_op jit(solution)/shard_map/all_gather | solution.py:121
  91.0 0.7 copy-start.8
  91.0 1.2 copy-start.7
  93.6 17.1 %all-to-all-start.2 = ((f32[32,2,128]{2,1,0:T(2,128)}), f32[32,2,128]{2,1,0:T(2,128)S(1)}, u32[]{:S(2)}, u32[]{:S(2)}) async-start(f32[32,2,128]{2,1,0:T(2,128)} %copy.121), calls=%async_computation.2 | async-start | bytes 65536 | tf_op jit(solution)/shard_map/all_to_all | solution.py:113
  121.1 2.9 copy-start.1
  157.9 4.4 %copy-start.2 = (bf16[32,1,2,128,128]{4,3,2,1,0:T(8,128)(2,1)}, bf16[32,1,2,128,128]{4,3,2,1,0:T(8,128)(2,1)S(1)}, u32[]{:S(2)}) copy-start(bf16[32,1,2,128,128]{4,3,2,1,0:T(8,128)(2,1)S(1)} %get-tuple-element.27) | copy-start | bytes 6291460
  316.2 19.4 %collective-permute-start.1 = (f32[32,128,128]{2,1,0:T(8,128)}, f32[32,128,128]{2,1,0:T(8,128)}, u32[]{:S(2)}, u32[]{:S(2)}) collective-permute-start(f32[32,128,128]{2,1,0:T(8,128)} %bitcast.110), channel_id=1, source_target_pairs={{0,1},{1,0},{2,3},{3,2},{4,5},{5,4},{6,7},{7,6},{8,9},{9,8},{10,11... | collective-permute-start | bytes 6291464 | tf_op jit(solution)/shard_map/ppermute | solution.py:133
  321.9 16.5 %collective-permute-start.2 = (f32[32,128,128]{2,1,0:T(8,128)}, f32[32,128,128]{2,1,0:T(8,128)}, u32[]{:S(2)}, u32[]{:S(2)}) collective-permute-start(f32[32,128,128]{2,1,0:T(8,128)} %bitcast.109), channel_id=1, source_target_pairs={{0,1},{1,0},{2,3},{3,2},{4,5},{5,4},{6,7},{7,6},{8,9},{9,8},{10,11... | collective-permute-start | bytes 6291464 | tf_op jit(solution)/shard_map/ppermute | solution.py:133
  325.5 47.5 %collective-permute-start = (f32[32,128,128]{2,1,0:T(8,128)}, f32[32,128,128]{2,1,0:T(8,128)}, u32[]{:S(2)}, u32[]{:S(2)}) collective-permute-start(f32[32,128,128]{2,1,0:T(8,128)} %dynamic-slice_bitcast_fusion), channel_id=1, source_target_pairs={{0,32},{32,0},{1,33},{33,1},{2,34},{34,2},{3,35},{35,3},{4,36},{36... | collective-permute-start | bytes 6291464 | tf_op jit(solution)/shard_map/ppermute | solution.py:133
  335.6 2.9 copy-start
  338.4 34.7 %copy-start.3 = (f32[8192,128]{1,0:T(8,128)S(1)}, f32[8192,128]{1,0:T(8,128)}, u32[]{:S(2)}) copy-start(f32[8192,128]{1,0:T(8,128)} %get-tuple-element.6) | copy-start | bytes 12582916
Sparse Core Ops, SparseCore 0:
  50.0 19.0 all-gather.7
  91.2 62.6 all-gather.5

commit v2 on v1

v2 whole, which is shorter than its diff:
```python
import functools

import jax
import jax.numpy as jnp
from jax import lax
from jax.experimental import pallas as pl
from jax.experimental.pallas import tpu as pltpu
from jax.sharding import Mesh, PartitionSpec as P

LOG2E = 1.4426950408889634
AXES = ('x1', 'x0', 'zh', 'zl', 'yh', 'yl', 'core')
N = 16
NA = 12
AHEAD = 2


def _kernel(scale, x4, st, out, qd, kv, qdt, kvt, sb, stb, dq, dkt, dvt, p_s, ds_s, dq_rx, dk_rx, dv_rx, stage, send, recv_qd, recv_kv, recv_st, fwd_send, fwd_qd, fwd_kv, fwd_st, x_send, x_dq, x_dk, x_dv, o_send, o_recv):
    f32, bf16 = jnp.float32, jnp.bfloat16
    R, D = x4.shape[2], x4.shape[3]
    BT = 4 * R
    x1, x0, zh, zl, yh, yl, core = [lax.axis_index(a) for a in AXES]
    xb = (x0 + x1) % 2

    def source(m):
        tx, ty, tzl, tzh = m % 2, m // 2 % 2, m // 4 % 2, m // 8
        sx = (x1 + tx) % 2
        return sx, (sx + xb) % 2, (zh + tzh) % 2, (zl + tzl) % 2, (yh + ty) % 2

    def device(m, u):
        sx, sx0, szh, szl, syh = source(m)
        return (sx, sx0, szh, szl, syh, (yl + u) % 2, core)

    def block(sx, syl):
        return syl + sx * (1 - 2 * syl)

    def place(m):
        sx, _, szh, szl, syh = source(m)
        zzy = 4 * szh + 2 * szl + syh
        return zzy + sx * (N - 1 - 2 * zzy)

    def head(dev):
        dx, _, dzh, dzl, dyh, dyl, _ = dev
        return (((dzh * 2 + dzl) * 2 + dyh) * 2 + dyl) * 2 + dx

    def chunk(m, b, i):
        return pl.ds(pl.multiple_of(m * BT + b * 2 * R + i * R, R), R)

    me = (x1, x0, zh, zl, yh, yl, core)
    x_peer = (x1, 1 - x0, zh, zl, yh, yl, core)
    c_peer = (x1, x0, zh, zl, yh, yl, 1 - core)
    my_b = block(x1, yl)

    def remote(src, dst, s_sem, r_sem, dev):
        return pltpu.make_async_remote_copy(src_ref=src, dst_ref=dst, send_sem=s_sem, recv_sem=r_sem, device_id=dev, device_id_type=pl.DeviceIdType.MESH)

    barrier = pltpu.get_barrier_semaphore()

    @pl.loop(1, 2 * N)
    def _(t):
        pl.semaphore_signal(barrier, inc=1, device_id=device(t // 2, t % 2), device_id_type=pl.DeviceIdType.MESH)

    for dev in (x_peer, c_peer):
        pl.semaphore_signal(barrier, inc=1, device_id=dev, device_id_type=pl.DeviceIdType.MESH)
    pl.semaphore_wait(barrier, 2 * N + 1)

    def parts(h, m, t):
        return (
            (x4.at[h, pl.ds(0, 2)], qd.at[:, chunk(m, my_b, x0)], send.at[0], recv_qd.at[t]),
            (x4.at[h, pl.ds(2, 2)], kv.at[:, chunk(m, my_b, core)], send.at[1], recv_kv.at[t]),
            (st.at[h], sb.at[:, chunk(m, my_b, x0)], send.at[2], recv_st.at[t]),
        )

    for src, dst, _, sem in parts(head(me), 0, 0):
        pltpu.make_async_copy(src, dst, sem).start()

    @pl.loop(1, 2 * N)
    def _(t):
        dev = device(t // 2, t % 2)
        for src, dst, ss, rs in parts(head(dev), t // 2, t):
            remote(src, dst, ss, rs, dev).start()

    def direct(m, u):
        sx, sx0, *_ = source(m)
        b = block(sx, (yl + u) % 2)
        return qd.at[:, chunk(m, b, sx0)], kv.at[:, chunk(m, b, core)], sb.at[:, chunk(m, b, sx0)]

    def passed(m, u):
        sx, sx0, *_ = source(m)
        b = block(sx, (yl + u) % 2)
        return qd.at[:, chunk(m, b, 1 - sx0)], kv.at[:, chunk(m, b, 1 - core)], sb.at[:, chunk(m, b, 1 - sx0)]

    def arrive(m):
        for u in range(2):
            t = 2 * m + u
            a, b, c = direct(m, u)
            pltpu.make_async_copy(a, a, recv_qd.at[t]).wait()
            remote(a, a, fwd_send.at[0], fwd_qd.at[t], x_peer).start()
            pltpu.make_async_copy(b, b, recv_kv.at[t]).wait()
            remote(b, b, fwd_send.at[1], fwd_kv.at[t], c_peer).start()
            pltpu.make_async_copy(c, c, recv_st.at[t]).wait()
            remote(c, c, fwd_send.at[2], fwd_st.at[t], x_peer).start()

    def rows(i):
        return pl.ds(pl.multiple_of(i * BT, BT), BT)

    def complete(m):
        for u in range(2):
            t = 2 * m + u
            a, b, c = passed(m, u)
            pltpu.make_async_copy(a, a, fwd_qd.at[t]).wait()
            pltpu.make_async_copy(b, b, fwd_kv.at[t]).wait()
            pltpu.make_async_copy(c, c, fwd_st.at[t]).wait()
        rs = rows(m)
        for i in range(2):
            qdt[i, :, rs] = qd[i, rs, :].T
            kvt[i, :, rs] = kv[i, rs, :].T
        stb[0, rs, :] = jnp.broadcast_to(sb[0:1, rs] * LOG2E, (128, BT)).T
        stb[1, rs, :] = jnp.broadcast_to(sb[1:2, rs], (128, BT)).T

    dkt[...] = jnp.zeros_like(dkt)
    dvt[...] = jnp.zeros_like(dvt)
    dq[...] = jnp.zeros_like(dq)
    p_s[1] = jnp.zeros((BT, BT), bf16)
    ds_s[1] = jnp.zeros((BT, BT), bf16)

    def stage1(qb, kb, slot, diag):
        qs, ks = rows(qb), rows(kb)
        s = jnp.dot(qd[0, qs, :], kvt[0, :, ks], preferred_element_type=f32)
        dp = jnp.dot(qd[1, qs, :], kvt[1, :, ks], preferred_element_type=f32)
        lb = jnp.tile(stb[0, qs, :], (1, BT // 128)) if BT >= 128 else stb[0, qs, :BT]
        db = jnp.tile(stb[1, qs, :], (1, BT // 128)) if BT >= 128 else stb[1, qs, :BT]
        p = jnp.exp2(s * (scale * LOG2E) - lb)
        if diag:
            hi = source(qb)[0]
            r = lax.broadcasted_iota(jnp.int32, (BT, BT), 0)
            c = lax.broadcasted_iota(jnp.int32, (BT, BT), 1)
            e = core + hi * (1 - 2 * core)
            qp = (r // (2 * R) * 2 + e) * (2 * R) + r % (2 * R)
            cc = c // R % 2
            half = xb + hi * (1 - 2 * xb)
            kp = (c // (2 * R) * 2 + cc + hi * (1 - 2 * cc)) * (2 * R) + half * R + c % R
            p = jnp.where(kp <= qp, p, 0.0)
        p_s[slot] = p.astype(bf16)
        ds_s[slot] = (p * (dp - db)).astype(bf16)

    def stage2(qb, kb, slot):
        qs, ks = rows(qb), rows(kb)
        dvt[:, ks] += jnp.dot(qdt[1, :, qs], p_s[slot], preferred_element_type=f32)
        dkt[:, ks] += jnp.dot(qdt[0, :, qs], ds_s[slot], preferred_element_type=f32)
        dq[qs, :] += jnp.dot(ds_s[slot], kv[0, ks, :], preferred_element_type=f32)

    def pair(i, j, carry):
        pq, pk, slot = carry
        late = (place(i) > place(j)).astype(jnp.int32)
        qb = j + late * (i - j)
        kb = i + j - qb
        stage2(pq, pk, 1 - slot)
        stage1(qb, kb, slot, False)
        return qb, kb, 1 - slot

    def same(i, carry):
        pq, pk, slot = carry
        stage2(pq, pk, 1 - slot)
        stage1(i, i, slot, True)
        return i, i, 1 - slot

    def swap(m):
        sx, sx0, *_ = source(m)
        for b in range(2):
            w = 2 * m + b
            a = chunk(m, b, 1 - sx0)
            c = chunk(m, b, 1 - core)
            remote(dq.at[a, :], dq_rx.at[w], x_send.at[0], x_dq.at[w], x_peer).start()
            remote(dkt.at[:, c], dk_rx.at[w], x_send.at[1], x_dk.at[w], c_peer).start()
            remote(dvt.at[:, c], dv_rx.at[w], x_send.at[2], x_dv.at[w], c_peer).start()

    def combine(m):
        sx, sx0, *_ = source(m)
        for b in range(2):
            w = 2 * m + b
            pltpu.make_async_copy(dq_rx.at[w], dq_rx.at[w], x_dq.at[w]).wait()
            pltpu.make_async_copy(dk_rx.at[w], dk_rx.at[w], x_dk.at[w]).wait()
            pltpu.make_async_copy(dv_rx.at[w], dv_rx.at[w], x_dv.at[w]).wait()
            a = chunk(m, b, sx0)
            c = chunk(m, b, core)
            stage[w, 0] = ((dq[a, :] + dq_rx[w]) * scale).astype(bf16)
            stage[w, 1] = ((dkt[:, c] + dk_rx[w]) * scale).T.astype(bf16)
            stage[w, 2] = (dvt[:, c] + dv_rx[w]).T.astype(bf16)

    def emit(m):
        sx, sx0, szh, szl, syh = source(m)
        for b in range(2):
            syl = block(sx, b)
            dev = (sx, sx0, szh, szl, syh, syl, core)
            own = jnp.logical_and(m == 0, syl == yl)

            @pl.when(own)
            def _():
                pltpu.make_async_copy(stage.at[2 * m + b], out.at[head(me)], o_send.at[1]).start()

            @pl.when(jnp.logical_not(own))
            def _():
                remote(stage.at[2 * m + b], out.at[head(me)], o_send.at[0], o_recv.at[0], dev).start()

    for m in range(AHEAD):
        arrive(m)

    def inflow(m, carry):
        @pl.when(m + AHEAD < N)
        def _():
            arrive(m + AHEAD)

        complete(m)
        carry = lax.fori_loop(0, m, lambda j, c: pair(m, j, c), carry)
        return same(m, carry)

    carry = lax.fori_loop(0, NA, inflow, (0, 0, 0))

    @pl.loop(NA, N)
    def _(m):
        @pl.when(m + AHEAD < N)
        def _():
            arrive(m + AHEAD)

        complete(m)

    def after(f):
        @pl.when(f >= 1)
        def _():
            swap(f - 1)

        @pl.when(f >= 2)
        def _():
            combine(f - 2)

        @pl.when(f >= 3)
        def _():
            emit(f - 3)

    def outflow(f, carry):
        carry = lax.fori_loop(NA, N, lambda j, c: pair(f, j, c), carry)
        after(f)
        return carry

    carry = lax.fori_loop(0, NA, outflow, carry)

    def last(f, carry):
        carry = same(f, carry)
        carry = lax.fori_loop(f + 1, N, lambda j, c: pair(f, j, c), carry)
        after(f)
        return carry

    pq, pk, slot = lax.fori_loop(NA, N, last, carry)
    stage2(pq, pk, 1 - slot)
    combine(N - 2)
    swap(N - 1)
    emit(N - 3)
    emit(N - 2)
    combine(N - 1)
    emit(N - 1)

    def drain(ref, sem):
        pltpu.make_async_copy(ref, ref, sem).wait()

    drain(x4.at[pl.ds(0, 2 * N - 1), pl.ds(0, 2)], send.at[0])
    drain(x4.at[pl.ds(0, 2 * N - 1), pl.ds(0, 2)], send.at[1])
    drain(st.at[pl.ds(0, 2 * N - 1)], send.at[2])
    drain(x4.at[pl.ds(0, 2 * N), pl.ds(0, 2)], fwd_send.at[0])
    drain(x4.at[pl.ds(0, 2 * N), pl.ds(0, 2)], fwd_send.at[1])
    drain(st.at[pl.ds(0, 2 * N)], fwd_send.at[2])
    drain(dq_rx, x_send.at[0])
    drain(dk_rx, x_send.at[1])
    drain(dv_rx, x_send.at[2])
    drain(stage.at[pl.ds(0, 2 * N - 1)], o_send.at[0])
    drain(stage.at[0], o_send.at[1])
    drain(stage.at[pl.ds(0, 2 * N - 1)], o_recv.at[0])


def _attention(x4, st, scale):
    h, _, r, d = x4.shape
    t = 4 * r * N
    f32, bf16, dma = jnp.float32, jnp.bfloat16, pltpu.SemaphoreType.DMA
    hbm = pl.BlockSpec(memory_space=pl.ANY)
    return pl.pallas_call(
        functools.partial(_kernel, scale),
        out_shape=jax.ShapeDtypeStruct((h, 3, r, d), bf16),
        in_specs=[hbm, hbm],
        out_specs=hbm,
        scratch_shapes=[
            pltpu.VMEM((2, t, d), bf16),
            pltpu.VMEM((2, t, d), bf16),
            pltpu.VMEM((2, d, t), bf16),
            pltpu.VMEM((2, d, t), bf16),
            pltpu.VMEM((2, t), f32),
            pltpu.VMEM((2, t, 128), f32),
            pltpu.VMEM((t, d), f32),
            pltpu.VMEM((d, t), f32),
            pltpu.VMEM((d, t), f32),
            pltpu.VMEM((2, 4 * r, 4 * r), bf16),
            pltpu.VMEM((2, 4 * r, 4 * r), bf16),
            pltpu.VMEM((h, r, d), f32),
            pltpu.VMEM((h, d, r), f32),
            pltpu.VMEM((h, d, r), f32),
            pltpu.VMEM((h, 3, r, d), bf16),
            dma((3,)), dma((h,)), dma((h,)), dma((h,)),
            dma((3,)), dma((h,)), dma((h,)), dma((h,)),
            dma((3,)), dma((h,)), dma((h,)), dma((h,)),
            dma((2,)), dma((1,)),
        ],
        compiler_params=pltpu.CompilerParams(collective_id=0, has_side_effects=True, vmem_limit_bytes=63 * 1024 * 1024),
        name='attn_bwd',
    )(x4, st)


def solution(mesh):
    fine = Mesh(mesh.devices.reshape((2,) * 7), AXES)
    rows = ('zh', 'zl', 'yh', 'yl', 'core', 'x1', 'x0')
    seq = P(None, rows, None, None)
    stat = P(None, None, rows)

    def body(q, k, v, o, do, lse):
        f32 = jnp.float32
        scale = q.shape[3] ** -0.5
        dlt = jnp.sum(do.astype(f32) * o.astype(f32), axis=-1)[0].T
        st = jnp.stack([lse[0], dlt], axis=1)
        x4 = jnp.stack([q[0], do[0], k[0], v[0]]).transpose(2, 0, 1, 3)
        out = _attention(x4, st, scale).transpose(1, 2, 0, 3)
        return out[0][None], out[1][None], out[2][None]

    return jax.shard_map(body, mesh=fine, in_specs=(seq, seq, seq, seq, seq, stat), out_specs=(seq, seq, seq), check_vma=False)
```

time: 444 us -> 197 us (0.44)
  blocking collectives: 132 us -> 0 us
  local copies, waits for them, and re-layouts: 87.2 us -> 11.5 us
  waiting for transfers between devices: 68 us -> 0 us
  Pallas kernels: 114 us -> 179 us
  between operations: 14.3 us -> 0.73 us
  starting transfers between devices: 12.1 us -> 0 us
  other arithmetic: 12.1 us -> 3.53 us
    all_to_all x3 -> x0, blocking collectives: 126 us -> none  [the longest x2 75.6 us: body(): lax.all_to_all(a, heads, 0, 0, tiled=True)]
    pallas_call x1, Pallas kernels: 114 us -> 179 us  [_attention(): pl.pallas_call(functools.partial(_kernel, scale), out_shape=jax.ShapeDtyp...]
    ppermute x3 -> x0, waiting for transfers between devices: 32.6 us -> none  [swap(): return mine + lax.ppermute(other, axis, [(0, 1), (1, 0)])]
    all_gather x2 -> x0, waiting for transfers between devices: 29.9 us -> none  [the longest x1 29.9 us: body(): qd = lax.all_gather(qd, 'xb', axis=2)]
    unnamed x30 -> x17, local copies, waits for them, and re-layouts: 31.3 us -> 9.24 us
    another operation x8 -> x0, local copies, waits for them, and re-layouts: 16.1 us -> none  [the longest x2 7.35 us: body(): qq, dd = [qd[:, i].reshape(t, d) for i in range(2)]]
    dynamic_slice x1 -> x0, local copies, waits for them, and re-layouts: 13.9 us -> none  [swap(): mine = lax.dynamic_index_in_dim(a, i, 1, keepdims=False)]
    reshape x2 -> x0, local copies, waits for them, and re-layouts: 13.1 us -> none  [the longest x1 6.58 us: body(): dv = swap(dvt.T.reshape(32, 2, r, d), 'core')]
  transfers between devices with their start and end apart: 6 -> 0, of which waited for: 3 -> 0; matrix products, arithmetic and copies ran while one was open for 8% -> 0% of each run, Pallas kernels for 0% -> 0%
where the time goes in v2:
time: 197 us; the launch traced here: 195 us
  Pallas kernels  179 us (91%)
  local copies, waits for them, and re-layouts  11.5 us (6%)
  other arithmetic  3.53 us (2%)
    pallas_call x1, Pallas kernels, _attention(): pl.pallas_call(functools.partial(_kernel, scale), out_shape=jax.ShapeDtyp...  179 us
    unnamed x17, local copies, waits for them, and re-layouts  9.24 us

profile of v2, /device:TPU:120, one launch (start us, length us, event | category | flops | bytes accessed | tf_op | source)
XLA Modules:
  0.0 194.6 jit_solution(15988683297738524984)
XLA Ops:
  0.6 0.0 copy-start.1
  0.6 0.0 copy-start.2
  0.7 1.8 copy.16
  2.4 1.6 copy.17
  4.1 0.0 copy-done.1
  4.1 0.4 copy.18
  4.5 0.0 copy-done.2
  4.5 0.4 copy.19
  4.9 0.0 copy-start
  4.9 0.0 copy-start.3
  4.9 0.0 copy-start.4
  5.0 2.2 %maximum_bitcast_fusion.x4 = bf16[32,4,128,128]{3,2,1,0:T(8,128)(2,1)} fusion(bf16[1,128,32,128]{3,1,0,2:T(8,128)(2,1)S(1)} %copy.19, bf16[1,128,32,128]{3,1,0,2:T(8,128)(2,1)S(1)} %copy.18, bf16[1,128,32,128]{3,1,0,2:T(8,128)(2,1)S(1)} %copy.17, bf16[1,128,32,128]{3,1,0,2:T(8,128)(2,1)S(1)} %copy.16), kind=kLoop, calls=%fused_computation | loop fusion | flops 6291456 | bytes 8388608 | tf_op jit(solution)/shard_map/transpose | solution.py:326
  7.2 0.0 copy-done
  7.2 0.0 copy-done.3
  7.2 0.6 multiply_reduce_fusion
  7.9 0.1 copy.20
  7.9 0.0 copy-done.4
  7.9 0.7 pad_maximum_fusion.st
  8.6 178.7 %attn_bwd.1 = bf16[32,3,128,128]{3,2,1,0:T(8,128)(2,1)} custom-call(bf16[32,4,128,128]{3,2,1,0:T(8,128)(2,1)} %maximum_bitcast_fusion.x4, f32[32,2,128]{2,1,0:T(2,128)} %pad_maximum_fusion.st), custom_call_target="tpu_custom_call" | custom-call | tf_op jit(solution)/shard_map/attn_bwd/pallas_call | solution.py:284
  187.3 2.3 %fusion = (bf16[1,128,32,128]{3,1,0,2:T(8,128)(2,1)S(1)}, bf16[1,128,32,128]{3,1,0,2:T(8,128)(2,1)S(1)}, bf16[1,128,32,128]{3,1,0,2:T(8,128)(2,1)S(1)}) fusion(bf16[3,128,32,128]{3,1,0,2:T(8,128)(2,1)} %bitcast.7), kind=kLoop, calls=%fused_computation.3 | loop fusion | bytes 6291456 | tf_op jit(solution)/shard_map/slice | solution.py:328
  189.6 1.6 copy.21
  191.3 1.6 copy.22
  192.9 1.6 copy.23
Async XLA Ops:
  0.6 3.4 %copy-start.1 = (bf16[1,128,32,128]{3,2,1,0:T(8,128)(2,1)S(1)}, bf16[1,128,32,128]{3,2,1,0:T(8,128)(2,1)}, u32[]{:S(2)}) copy-start(bf16[1,128,32,128]{3,2,1,0:T(8,128)(2,1)} %param.7) | copy-start | bytes 3145732
  0.6 3.9 %copy-start.2 = (bf16[1,128,32,128]{3,2,1,0:T(8,128)(2,1)S(1)}, bf16[1,128,32,128]{3,2,1,0:T(8,128)(2,1)}, u32[]{:S(2)}) copy-start(bf16[1,128,32,128]{3,2,1,0:T(8,128)(2,1)} %param.8) | copy-start | bytes 3145732
  4.9 2.3 %copy-start = (bf16[1,128,32,128]{3,2,1,0:T(8,128)(2,1)S(1)}, bf16[1,128,32,128]{3,2,1,0:T(8,128)(2,1)}, u32[]{:S(2)}) copy-start(bf16[1,128,32,128]{3,2,1,0:T(8,128)(2,1)} %param.10) | copy-start | bytes 3145732
  4.9 2.3 %copy-start.3 = (bf16[1,128,32,128]{3,2,1,0:T(8,128)(2,1)S(1)}, bf16[1,128,32,128]{3,2,1,0:T(8,128)(2,1)}, u32[]{:S(2)}) copy-start(bf16[1,128,32,128]{3,2,1,0:T(8,128)(2,1)} %param.9) | copy-start | bytes 3145732
  4.9 3.0 %copy-start.4 = (f32[1,32,128]{2,1,0:T(8,128)S(1)}, f32[1,32,128]{2,1,0:T(8,128)}, u32[]{:S(2)}) copy-start(f32[1,32,128]{2,1,0:T(8,128)} %param.11) | copy-start | bytes 49156

commit v3 on v2

v3 whole, which is shorter than its diff:
```python
import functools

import jax
import jax.numpy as jnp
from jax import lax
from jax.experimental import pallas as pl
from jax.experimental.pallas import tpu as pltpu
from jax.sharding import Mesh, PartitionSpec as P

LOG2E = 1.4426950408889634
AXES = ('x1', 'x0', 'zh', 'zl', 'yh', 'yl', 'core')
N = 16
NA = 10
NF = 5
AHEAD = 1
FIRST = 4


def _kernel(scale, qh, doh, kh, vh, st, out_q, out_k, out_v, qd, kv, qdt, kvt, sb, stb, dq, dkt, dvt, p_s, ds_s, dst_s, dq_rx, dk_rx, dv_rx, stage, send, recv_qd, recv_kv, recv_st, fwd_send, fwd_qd, fwd_kv, fwd_st, x_send, x_dq, x_dk, x_dv, o_send, o_recv):
    f32, bf16 = jnp.float32, jnp.bfloat16
    R = qh.shape[1]
    BT = 4 * R
    x1, x0, zh, zl, yh, yl, core = [lax.axis_index(a) for a in AXES]
    xb = (x0 + x1) % 2

    def source(m):
        a, b, c, d = m % 2, m // 2 % 2, m // 4 % 2, m // 8
        tx, ty, tzl, tzh = (a + b) % 2, (a + c) % 2, d, a
        sx = (x1 + tx) % 2
        return sx, (sx + xb) % 2, (zh + tzh) % 2, (zl + tzl) % 2, (yh + ty) % 2

    def device(m, u):
        sx, sx0, szh, szl, syh = source(m)
        return (sx, sx0, szh, szl, syh, (yl + u) % 2, core)

    def block(sx, syl):
        return syl + sx * (1 - 2 * syl)

    def place(m):
        sx, _, szh, szl, syh = source(m)
        zzy = 4 * szh + 2 * szl + syh
        return zzy + sx * (N - 1 - 2 * zzy)

    def head(dev):
        dx, _, dzh, dzl, dyh, dyl, _ = dev
        return (((dzh * 2 + dzl) * 2 + dyh) * 2 + dyl) * 2 + dx

    def chunk(m, b, i):
        return pl.ds(pl.multiple_of(m * BT + b * 2 * R + i * R, R), R)

    me = (x1, x0, zh, zl, yh, yl, core)
    x_peer = (x1, 1 - x0, zh, zl, yh, yl, core)
    c_peer = (x1, x0, zh, zl, yh, yl, 1 - core)
    my_b = block(x1, yl)

    def remote(src, dst, s_sem, r_sem, dev):
        return pltpu.make_async_remote_copy(src_ref=src, dst_ref=dst, send_sem=s_sem, recv_sem=r_sem, device_id=dev, device_id_type=pl.DeviceIdType.MESH)

    barrier = pltpu.get_barrier_semaphore()

    @pl.loop(1, 2 * N)
    def _(t):
        pl.semaphore_signal(barrier, inc=1, device_id=device(t // 2, t % 2), device_id_type=pl.DeviceIdType.MESH)

    for dev in (x_peer, c_peer):
        pl.semaphore_signal(barrier, inc=1, device_id=dev, device_id_type=pl.DeviceIdType.MESH)
    pl.semaphore_wait(barrier, 2 * N + 1)

    def parts(h, m, t):
        a, b = chunk(m, my_b, x0), chunk(m, my_b, core)
        return (
            (qh.at[h], qd.at[0, a, :], send.at[0], recv_qd.at[t]),
            (doh.at[h], qd.at[1, a, :], send.at[0], recv_qd.at[t]),
            (kh.at[h], kv.at[0, b, :], send.at[1], recv_kv.at[t]),
            (vh.at[h], kv.at[1, b, :], send.at[1], recv_kv.at[t]),
            (st.at[h], sb.at[:, a], send.at[2], recv_st.at[t]),
        )

    for src, dst, _, sem in parts(head(me), 0, 0):
        pltpu.make_async_copy(src, dst, sem).start()

    def issue(m):
        for u in range(2):
            @pl.when(2 * m + u > 0)
            def _():
                dev = device(m, u)
                for src, dst, ss, rs in parts(head(dev), m, 2 * m + u):
                    remote(src, dst, ss, rs, dev).start()

    @pl.loop(0, FIRST)
    def _(m):
        issue(m)

    def direct(m, u):
        sx, sx0, *_ = source(m)
        b = block(sx, (yl + u) % 2)
        return qd.at[:, chunk(m, b, sx0)], kv.at[:, chunk(m, b, core)], sb.at[:, chunk(m, b, sx0)]

    def passed(m, u):
        sx, sx0, *_ = source(m)
        b = block(sx, (yl + u) % 2)
        return qd.at[:, chunk(m, b, 1 - sx0)], kv.at[:, chunk(m, b, 1 - core)], sb.at[:, chunk(m, b, 1 - sx0)]

    def arrive(m):
        for u in range(2):
            t = 2 * m + u
            a, b, c = direct(m, u)
            pltpu.make_async_copy(a, a, recv_qd.at[t]).wait()
            remote(a, a, fwd_send.at[0], fwd_qd.at[t], x_peer).start()
            pltpu.make_async_copy(b, b, recv_kv.at[t]).wait()
            remote(b, b, fwd_send.at[1], fwd_kv.at[t], c_peer).start()
            pltpu.make_async_copy(c, c, recv_st.at[t]).wait()
            remote(c, c, fwd_send.at[2], fwd_st.at[t], x_peer).start()

        @pl.loop(FIRST + 2 * m, FIRST + 2 * m + 2)
        def _(w):
            @pl.when(w < N)
            def _():
                issue(w)

    def rows(i):
        return pl.ds(pl.multiple_of(i * BT, BT), BT)

    def complete(m):
        for u in range(2):
            t = 2 * m + u
            a, b, c = passed(m, u)
            pltpu.make_async_copy(a, a, fwd_qd.at[t]).wait()
            pltpu.make_async_copy(b, b, fwd_kv.at[t]).wait()
            pltpu.make_async_copy(c, c, fwd_st.at[t]).wait()
        rs = rows(m)
        for i in range(2):
            qdt[i, :, rs] = qd[i, rs, :].T
            kvt[i, :, rs] = kv[i, rs, :].T
        stb[0, rs, :] = jnp.broadcast_to(sb[0:1, rs] * LOG2E, (128, BT)).T
        stb[1, rs, :] = jnp.broadcast_to(sb[1:2, rs], (128, BT)).T

    dkt[...] = jnp.zeros_like(dkt)
    dvt[...] = jnp.zeros_like(dvt)
    dq[...] = jnp.zeros_like(dq)
    p_s[1] = jnp.zeros((BT, BT), bf16)
    ds_s[1] = jnp.zeros((BT, BT), bf16)
    dst_s[1] = jnp.zeros((BT, BT), bf16)

    def stage1(qb, kb, slot, diag):
        ks = rows(kb)
        for g in range(2):
            gs = pl.ds(pl.multiple_of(qb * BT + g * 2 * R, 2 * R), 2 * R)
            go = pl.ds(g * 2 * R, 2 * R)
            s = jnp.dot(qd[0, gs, :], kvt[0, :, ks], preferred_element_type=f32)
            dp = jnp.dot(qd[1, gs, :], kvt[1, :, ks], preferred_element_type=f32)
            lb, db = [jnp.tile(stb[i, gs, :], (1, BT // 128)) if BT >= 128 else stb[i, gs, :BT] for i in range(2)]
            p = jnp.exp2(s * (scale * LOG2E) - lb)
            if diag:
                hi = source(qb)[0]
                r = lax.broadcasted_iota(jnp.int32, p.shape, 0)
                c = lax.broadcasted_iota(jnp.int32, p.shape, 1)
                qp = (g * 2 + core + hi * (1 - 2 * core)) * (2 * R) + r
                cc = c // R % 2
                half = xb + hi * (1 - 2 * xb)
                kp = (c // (2 * R) * 2 + cc + hi * (1 - 2 * cc)) * (2 * R) + half * R + c % R
                p = jnp.where(kp <= qp, p, 0.0)
            p_s[slot, go, :] = p.astype(bf16)
            ds = (p * (dp - db)).astype(bf16)
            ds_s[slot, go, :] = ds
            dst_s[slot, :, go] = ds.T

    def stage2(qb, kb, slot):
        qs, ks = rows(qb), rows(kb)
        dvt[:, ks] += jnp.dot(qdt[1, :, qs], p_s[slot], preferred_element_type=f32)
        dkt[:, ks] += jnp.dot(qdt[0, :, qs], ds_s[slot], preferred_element_type=f32)
        dq[:, qs] += jnp.dot(kvt[0, :, ks], dst_s[slot], preferred_element_type=f32)

    def rank(i, j):
        late = (place(i) > place(j)).astype(jnp.int32)
        qb = j + late * (i - j)
        return qb, i + j - qb

    def two(i, j, carry):
        a, b = rank(i, j), rank(i, j + 1)
        stage2(*carry, 1)
        stage1(*a, 0, False)
        stage1(*b, 1, False)
        stage2(*a, 0)
        return b

    def diagonal(i, j, with_pair, carry):
        @pl.when(with_pair)
        def _():
            a = rank(i, j)
            stage2(*carry, 1)
            stage1(*a, 0, False)
            stage1(i, i, 1, True)
            stage2(*a, 0)

        @pl.when(jnp.logical_not(with_pair))
        def _():
            stage2(*carry, 1)
            stage1(i, i, 1, True)

        return i, i

    def swap(m):
        sx, sx0, *_ = source(m)
        for b in range(2):
            w = 2 * m + b
            a = chunk(m, b, 1 - sx0)
            c = chunk(m, b, 1 - core)
            remote(dq.at[:, a], dq_rx.at[w], x_send.at[0], x_dq.at[w], x_peer).start()
            remote(dkt.at[:, c], dk_rx.at[w], x_send.at[1], x_dk.at[w], c_peer).start()
            remote(dvt.at[:, c], dv_rx.at[w], x_send.at[2], x_dv.at[w], c_peer).start()

    def combine(m):
        sx, sx0, *_ = source(m)
        for b in range(2):
            w = 2 * m + b
            pltpu.make_async_copy(dq_rx.at[w], dq_rx.at[w], x_dq.at[w]).wait()
            pltpu.make_async_copy(dk_rx.at[w], dk_rx.at[w], x_dk.at[w]).wait()
            pltpu.make_async_copy(dv_rx.at[w], dv_rx.at[w], x_dv.at[w]).wait()
            a = chunk(m, b, sx0)
            c = chunk(m, b, core)
            stage[w, 0] = ((dq[:, a] + dq_rx[w]) * scale).T.astype(bf16)
            stage[w, 1] = ((dkt[:, c] + dk_rx[w]) * scale).T.astype(bf16)
            stage[w, 2] = (dvt[:, c] + dv_rx[w]).T.astype(bf16)

    def emit(m):
        sx, sx0, szh, szl, syh = source(m)
        for b in range(2):
            syl = block(sx, b)
            dev = (sx, sx0, szh, szl, syh, syl, core)
            own = jnp.logical_and(m == 0, syl == yl)
            ends = [(stage.at[2 * m + b, i], o.at[head(me)]) for i, o in enumerate((out_q, out_k, out_v))]

            @pl.when(own)
            def _():
                for src, dst in ends:
                    pltpu.make_async_copy(src, dst, o_send.at[1]).start()

            @pl.when(jnp.logical_not(own))
            def _():
                for src, dst in ends:
                    remote(src, dst, o_send.at[0], o_recv.at[0], dev).start()

    for m in range(AHEAD):
        arrive(m)

    def inflow(m, carry):
        count = 1 + (m >= NF).astype(jnp.int32)
        first = m + AHEAD + (m - NF) * (count - 1)

        @pl.loop(0, count)
        def _(i):
            @pl.when(first + i < N)
            def _():
                arrive(first + i)

        complete(m)
        carry = diagonal(m, m - 1, m % 2 == 1, carry)
        return lax.fori_loop(0, m // 2, lambda j, c: two(m, 2 * j, c), carry)

    carry = lax.fori_loop(0, NA, inflow, (0, 0))

    @pl.loop(NA, N)
    def _(m):
        complete(m)

    def outflow(f, carry):
        def step(j, carry):
            carry = two(f, NA + 2 * j, carry)

            @pl.when(jnp.logical_and(j == 0, f >= 1))
            def _():
                swap(f - 1)

            @pl.when(jnp.logical_and(j == 1, f >= 2))
            def _():
                combine(f - 2)

            @pl.when(jnp.logical_and(j == 2, f >= 2))
            def _():
                emit(f - 2)

            return carry

        return lax.fori_loop(0, (N - NA) // 2, step, carry)

    carry = lax.fori_loop(0, NA, outflow, carry)

    def last(f, carry):
        carry = diagonal(f, N - 1, f % 2 == 0, carry)
        swap(f - 1)

        @pl.when(f > NA)
        def _():
            emit(f - 3)

        carry = lax.fori_loop(0, (N - 1 - f) // 2, lambda j, c: two(f, f + 1 + 2 * j, c), carry)
        combine(f - 2)
        return carry

    carry = lax.fori_loop(NA, N, last, carry)
    stage2(*carry, 1)
    emit(N - 3)
    swap(N - 1)
    combine(N - 2)
    emit(N - 2)
    combine(N - 1)
    emit(N - 1)

    def drain(ref, sem):
        pltpu.make_async_copy(ref, ref, sem).wait()

    drain(stage.at[pl.ds(0, 2 * N - 1), pl.ds(0, 2)], send.at[0])
    drain(stage.at[pl.ds(0, 2 * N - 1), pl.ds(0, 2)], send.at[1])
    drain(st.at[pl.ds(0, 2 * N - 1)], send.at[2])
    drain(stage.at[pl.ds(0, 2 * N), pl.ds(0, 2)], fwd_send.at[0])
    drain(stage.at[pl.ds(0, 2 * N), pl.ds(0, 2)], fwd_send.at[1])
    drain(st.at[pl.ds(0, 2 * N)], fwd_send.at[2])
    drain(dq_rx, x_send.at[0])
    drain(dk_rx, x_send.at[1])
    drain(dv_rx, x_send.at[2])
    drain(stage.at[pl.ds(0, 2 * N - 1)], o_send.at[0])
    drain(stage.at[0], o_send.at[1])
    drain(stage.at[pl.ds(0, 2 * N - 1)], o_recv.at[0])


def _attention(qh, doh, kh, vh, st, scale):
    h, r, d = qh.shape
    t = 4 * r * N
    f32, bf16, dma = jnp.float32, jnp.bfloat16, pltpu.SemaphoreType.DMA
    hbm = pl.BlockSpec(memory_space=pl.ANY)
    return pl.pallas_call(
        functools.partial(_kernel, scale),
        out_shape=(jax.ShapeDtypeStruct((h, r, d), bf16),) * 3,
        in_specs=[hbm] * 5,
        out_specs=(hbm,) * 3,
        scratch_shapes=[
            pltpu.VMEM((2, t, d), bf16),
            pltpu.VMEM((2, t, d), bf16),
            pltpu.VMEM((2, d, t), bf16),
            pltpu.VMEM((2, d, t), bf16),
            pltpu.VMEM((2, t), f32),
            pltpu.VMEM((2, t, 128), f32),
            pltpu.VMEM((d, t), f32),
            pltpu.VMEM((d, t), f32),
            pltpu.VMEM((d, t), f32),
            pltpu.VMEM((2, 4 * r, 4 * r), bf16),
            pltpu.VMEM((2, 4 * r, 4 * r), bf16),
            pltpu.VMEM((2, 4 * r, 4 * r), bf16),
            pltpu.VMEM((h, d, r), f32),
            pltpu.VMEM((h, d, r), f32),
            pltpu.VMEM((h, d, r), f32),
            pltpu.VMEM((h, 3, r, d), bf16),
            dma((3,)), dma((h,)), dma((h,)), dma((h,)),
            dma((3,)), dma((h,)), dma((h,)), dma((h,)),
            dma((3,)), dma((h,)), dma((h,)), dma((h,)),
            dma((2,)), dma((1,)),
        ],
        compiler_params=pltpu.CompilerParams(collective_id=0, has_side_effects=True, vmem_limit_bytes=63 * 1024 * 1024),
        name='attn_bwd',
    )(qh, doh, kh, vh, st)


def solution(mesh):
    fine = Mesh(mesh.devices.reshape((2,) * 7), AXES)
    rows = ('zh', 'zl', 'yh', 'yl', 'core', 'x1', 'x0')
    seq = P(None, rows, None, None)
    stat = P(None, None, rows)

    def body(q, k, v, o, do, lse):
        f32 = jnp.float32
        scale = q.shape[3] ** -0.5
        dlt = jnp.sum(do.astype(f32) * o.astype(f32), axis=-1)[0].T
        st = jnp.stack([lse[0], dlt], axis=1)
        grads = _attention(*[a[0].transpose(1, 0, 2) for a in (q, do, k, v)], st, scale)
        return tuple(g.transpose(1, 0, 2)[None] for g in grads)

    return jax.shard_map(body, mesh=fine, in_specs=(seq, seq, seq, seq, seq, stat), out_specs=(seq, seq, seq), check_vma=False)
```

time: 197 us -> 167 us (0.85)
  the two profiles are of different devices: /device:TPU:120 before, /device:TPU:39 now
where the time goes in v3:
time: 167 us
  Pallas kernels  152 us (91%)
  local copies, waits for them, and re-layouts  10.6 us (6%)
  other arithmetic  2.96 us (2%)
    pallas_call x1, Pallas kernels, _attention(): pl.pallas_call(functools.partial(_kernel, scale), out_shape=(jax.ShapeDty...  152 us
    unnamed x17, local copies, waits for them, and re-layouts  6.29 us
    transpose x2, local copies, waits for them, and re-layouts, body(): a[0].transpose(1, 0, 2)  4.25 us

profile of v3, /device:TPU:39, one launch (start us, length us, event | category | flops | bytes accessed | tf_op | source)
XLA Modules:
  0.0 166.5 jit_solution(10734904484965348510)
XLA Ops:
  0.6 0.0 copy-start.6
  0.6 0.0 copy-start
  0.7 0.0 copy-start.3
  0.7 2.3 %multiply_reduce_fusion = f32[128,32]{1,0:T(8,128)S(1)} fusion(bf16[1,128,32,128]{3,2,1,0:T(8,128)(2,1)} %param.9, bf16[1,128,32,128]{3,2,1,0:T(8,128)(2,1)} %param.10), kind=kLoop, calls=%fused_computation | loop fusion | flops 2093056 | bytes 2113536 | tf_op jit(solution)/shard_map/reduce_sum | solution.py:373
  3.0 0.1 copy.20
  3.0 0.0 copy-done.6
  3.0 0.7 pad_maximum_fusion.st
  3.7 0.0 copy-done
  3.7 0.0 copy-done.3
  3.7 0.0 copy-start.4
  3.7 0.0 copy-start.5
  3.7 2.1 %copy_bitcast_fusion.2 = (bf16[32,128,128]{2,1,0:T(8,128)(2,1)}, bf16[32,128,128]{2,1,0:T(8,128)(2,1)}) fusion(bf16[1,128,32,128]{3,2,1,0:T(8,128)(2,1)S(1)} %copy-done, bf16[1,128,32,128]{3,2,1,0:T(8,128)(2,1)S(1)} %copy-done.3), kind=kLoop, calls=%fused_computation.3 | loop fusion | bytes 4194304 | tf_op jit(solution)/shard_map/transpose | solution.py:375
  5.8 0.0 copy-done.4
  5.8 0.0 copy-done.5
  5.8 2.1 %copy_bitcast_fusion = (bf16[32,128,128]{2,1,0:T(8,128)(2,1)}, bf16[32,128,128]{2,1,0:T(8,128)(2,1)}) fusion(bf16[1,128,32,128]{3,2,1,0:T(8,128)(2,1)S(1)} %copy-done.4, bf16[1,128,32,128]{3,2,1,0:T(8,128)(2,1)S(1)} %copy-done.5), kind=kLoop, calls=%fused_computation.1 | loop fusion | bytes 4194304 | tf_op jit(solution)/shard_map/transpose | solution.py:375
  8.0 152.3 %attn_bwd.1 = (bf16[32,128,128]{2,1,0:T(8,128)(2,1)}, bf16[32,128,128]{2,1,0:T(8,128)(2,1)}, bf16[32,128,128]{2,1,0:T(8,128)(2,1)}) custom-call(bf16[32,128,128]{2,1,0:T(8,128)(2,1)} %get-tuple-element.18.qh, bf16[32,128,128]{2,1,0:T(8,128)(2,1)} %get-tuple-element.17.doh, bf16[32,128,128]{2,1,0:T(8,128)(2,1)} %get-tuple-element.16.kh, ...), custom_call_target="tpu_custom_call" | custom-call | tf_op jit(solution)/shard_map/attn_bwd/pallas_call | solution.py:332
  160.2 0.0 copy-start.2
  160.2 3.0 %copy.21 = bf16[1,128,32,128]{3,2,1,0:T(8,128)(2,1)} copy(bf16[1,128,32,128]{3,1,2,0:T(8,128)(2,1)} %bitcast.31) | data formatting | bytes 2097152
  163.2 0.0 copy-done.2
  163.2 0.0 copy-start.1
  163.2 1.6 copy.22
  164.9 0.0 copy-done.1
  164.9 1.6 copy.23
Async XLA Ops:
  0.6 2.4 %copy-start.6 = (f32[1,32,128]{2,1,0:T(8,128)S(1)}, f32[1,32,128]{2,1,0:T(8,128)}, u32[]{:S(2)}) copy-start(f32[1,32,128]{2,1,0:T(8,128)} %param.11) | copy-start | bytes 49156
  0.6 3.0 %copy-start = (bf16[1,128,32,128]{3,2,1,0:T(8,128)(2,1)S(1)}, bf16[1,128,32,128]{3,2,1,0:T(8,128)(2,1)}, u32[]{:S(2)}) copy-start(bf16[1,128,32,128]{3,2,1,0:T(8,128)(2,1)} %param.10) | copy-start | bytes 3145732
  0.7 3.0 %copy-start.3 = (bf16[1,128,32,128]{3,2,1,0:T(8,128)(2,1)S(1)}, bf16[1,128,32,128]{3,2,1,0:T(8,128)(2,1)}, u32[]{:S(2)}) copy-start(bf16[1,128,32,128]{3,2,1,0:T(8,128)(2,1)} %param.6) | copy-start | bytes 3145732
  3.7 2.1 %copy-start.4 = (bf16[1,128,32,128]{3,2,1,0:T(8,128)(2,1)S(1)}, bf16[1,128,32,128]{3,2,1,0:T(8,128)(2,1)}, u32[]{:S(2)}) copy-start(bf16[1,128,32,128]{3,2,1,0:T(8,128)(2,1)} %param.8) | copy-start | bytes 3145732
  3.7 2.1 %copy-start.5 = (bf16[1,128,32,128]{3,2,1,0:T(8,128)(2,1)S(1)}, bf16[1,128,32,128]{3,2,1,0:T(8,128)(2,1)}, u32[]{:S(2)}) copy-start(bf16[1,128,32,128]{3,2,1,0:T(8,128)(2,1)} %param.7) | copy-start | bytes 3145732
  160.2 3.0 %copy-start.2 = (bf16[32,128,128]{2,1,0:T(8,128)(2,1)S(1)}, bf16[32,128,128]{2,1,0:T(8,128)(2,1)}, u32[]{:S(2)}) copy-start(bf16[32,128,128]{2,1,0:T(8,128)(2,1)} %get-tuple-element.7) | copy-start | bytes 3145732
  163.2 1.7 copy-start.1

commit v4 on v3

--- a/solution.py
+++ b/solution.py
@@ -10,10 +10,12 @@
 LOG2E = 1.4426950408889634
 AXES = ('x1', 'x0', 'zh', 'zl', 'yh', 'yl', 'core')
 N = 16
-NA = 10
-NF = 5
+NA = 12
+NF = 8
 AHEAD = 1
 FIRST = 4
+NS = 3
+LAG = 4
 
 
 def _kernel(scale, qh, doh, kh, vh, st, out_q, out_k, out_v, qd, kv, qdt, kvt, sb, stb, dq, dkt, dvt, p_s, ds_s, dst_s, dq_rx, dk_rx, dv_rx, stage, send, recv_qd, recv_kv, recv_st, fwd_send, fwd_qd, fwd_kv, fwd_st, x_send, x_dq, x_dk, x_dv, o_send, o_recv):
@@ -112,7 +114,10 @@
             pltpu.make_async_copy(c, c, recv_st.at[t]).wait()
             remote(c, c, fwd_send.at[2], fwd_st.at[t], x_peer).start()
 
-        @pl.loop(FIRST + 2 * m, FIRST + 2 * m + 2)
+        more = (m >= NS).astype(jnp.int32)
+        w0 = FIRST + m + more * (m - NS)
+
+        @pl.loop(w0, w0 + 1 + more)
         def _(w):
             @pl.when(w < N)
             def _():
@@ -184,6 +189,19 @@
         stage2(*a, 0)
         return b
 
+    def four(i, j, carry, extra=lambda: None):
+        a, b, c, d = [rank(i, j + n) for n in range(4)]
+        stage2(*carry, 1)
+        stage1(*a, 0, False)
+        stage1(*b, 1, False)
+        stage2(*a, 0)
+        stage2(*b, 1)
+        extra()
+        stage1(*c, 0, False)
+        stage1(*d, 1, False)
+        stage2(*c, 0)
+        return d
+
     def diagonal(i, j, with_pair, carry):
         @pl.when(with_pair)
         def _():
@@ -210,13 +228,16 @@
             remote(dkt.at[:, c], dk_rx.at[w], x_send.at[1], x_dk.at[w], c_peer).start()
             remote(dvt.at[:, c], dv_rx.at[w], x_send.at[2], x_dv.at[w], c_peer).start()
 
+    def swapped(m):
+        for b in range(2):
+            w = 2 * m + b
+            for ref, sem in ((dq_rx, x_dq), (dk_rx, x_dk), (dv_rx, x_dv)):
+                pltpu.make_async_copy(ref.at[w], ref.at[w], sem.at[w]).wait()
+
     def combine(m):
         sx, sx0, *_ = source(m)
         for b in range(2):
             w = 2 * m + b
-            pltpu.make_async_copy(dq_rx.at[w], dq_rx.at[w], x_dq.at[w]).wait()
-            pltpu.make_async_copy(dk_rx.at[w], dk_rx.at[w], x_dk.at[w]).wait()
-            pltpu.make_async_copy(dv_rx.at[w], dv_rx.at[w], x_dv.at[w]).wait()
             a = chunk(m, b, sx0)
             c = chunk(m, b, core)
             stage[w, 0] = ((dq[:, a] + dq_rx[w]) * scale).T.astype(bf16)
@@ -241,7 +262,8 @@
                 for src, dst in ends:
                     remote(src, dst, o_send.at[0], o_recv.at[0], dev).start()
 
-    for m in range(AHEAD):
+    @pl.loop(0, AHEAD)
+    def _(m):
         arrive(m)
 
     def inflow(m, carry):
@@ -255,8 +277,16 @@
                 arrive(first + i)
 
         complete(m)
+        j = m // 4 * 4
+        some = m // 2 % 2 == 1
+
+        @pl.when(some)
+        def _():
+            two(m, j, carry)
+
+        carry = [jnp.where(some, a, b) for a, b in zip(rank(m, j + 1), carry)]
         carry = diagonal(m, m - 1, m % 2 == 1, carry)
-        return lax.fori_loop(0, m // 2, lambda j, c: two(m, 2 * j, c), carry)
+        return lax.fori_loop(0, m // 4, lambda j, c: four(m, 4 * j, c), carry)
 
     carry = lax.fori_loop(0, NA, inflow, (0, 0))
 
@@ -265,47 +295,44 @@
         complete(m)
 
     def outflow(f, carry):
-        def step(j, carry):
-            carry = two(f, NA + 2 * j, carry)
-
-            @pl.when(jnp.logical_and(j == 0, f >= 1))
-            def _():
-                swap(f - 1)
-
-            @pl.when(jnp.logical_and(j == 1, f >= 2))
-            def _():
-                combine(f - 2)
-
-            @pl.when(jnp.logical_and(j == 2, f >= 2))
-            def _():
-                emit(f - 2)
-
-            return carry
-
-        return lax.fori_loop(0, (N - NA) // 2, step, carry)
-
-    carry = lax.fori_loop(0, NA, outflow, carry)
+        carry = four(f, NA, carry)
+
+        @pl.when(f >= 1)
+        def _():
+            swap(f - 1)
+
+        return carry
+
+    def outflow_sums(f, carry):
+        swapped(f - LAG)
+        carry = four(f, NA, carry, lambda: combine(f - LAG))
+        swap(f - 1)
+        emit(f - LAG)
+        return carry
+
+    def finish(m):
+        swapped(m)
+        combine(m)
+        emit(m)
+
+    carry = lax.fori_loop(0, LAG, outflow, carry)
+    carry = lax.fori_loop(LAG, NA, outflow_sums, carry)
+    finish(NA - LAG)
 
     def last(f, carry):
         carry = diagonal(f, N - 1, f % 2 == 0, carry)
         swap(f - 1)
-
-        @pl.when(f > NA)
-        def _():
-            emit(f - 3)
-
         carry = lax.fori_loop(0, (N - 1 - f) // 2, lambda j, c: two(f, f + 1 + 2 * j, c), carry)
-        combine(f - 2)
+        finish(f + 1 - LAG)
         return carry
 
     carry = lax.fori_loop(NA, N, last, carry)
     stage2(*carry, 1)
-    emit(N - 3)
     swap(N - 1)
-    combine(N - 2)
-    emit(N - 2)
-    combine(N - 1)
-    emit(N - 1)
+
+    @pl.loop(N + 1 - LAG, N)
+    def _(m):
+        finish(m)
 
     def drain(ref, sem):
         pltpu.make_async_copy(ref, ref, sem).wait()

time: 167 us -> 161 us (0.964)
  the two profiles are of different devices: /device:TPU:39 before, /device:TPU:4 now
where the time goes in v4:
time: 161 us
  Pallas kernels  146 us (91%)
  local copies, waits for them, and re-layouts  10.6 us (7%)
  other arithmetic  2.96 us (2%)
    pallas_call x1, Pallas kernels, _attention(): pl.pallas_call(functools.partial(_kernel, scale), out_shape=(jax.ShapeDty...  146 us
    unnamed x17, local copies, waits for them, and re-layouts  6.29 us
    transpose x2, local copies, waits for them, and re-layouts, body(): a[0].transpose(1, 0, 2)  4.25 us

profile of v4, /device:TPU:4, one launch (start us, length us, event | category | flops | bytes accessed | tf_op | source)
XLA Modules:
  0.0 160.7 jit_solution(14350686765259667120)
XLA Ops:
  0.6 0.0 copy-start.6
  0.6 0.0 copy-start
  0.7 0.0 copy-start.3
  0.7 2.3 %multiply_reduce_fusion = f32[128,32]{1,0:T(8,128)S(1)} fusion(bf16[1,128,32,128]{3,2,1,0:T(8,128)(2,1)} %param.9, bf16[1,128,32,128]{3,2,1,0:T(8,128)(2,1)} %param.10), kind=kLoop, calls=%fused_computation | loop fusion | flops 2093056 | bytes 2113536 | tf_op jit(solution)/shard_map/reduce_sum | solution.py:400
  3.0 0.1 copy.20
  3.0 0.0 copy-done.6
  3.0 0.7 pad_maximum_fusion.st
  3.7 0.0 copy-done
  3.7 0.0 copy-done.3
  3.7 0.0 copy-start.4
  3.7 0.0 copy-start.5
  3.7 2.1 %copy_bitcast_fusion.2 = (bf16[32,128,128]{2,1,0:T(8,128)(2,1)}, bf16[32,128,128]{2,1,0:T(8,128)(2,1)}) fusion(bf16[1,128,32,128]{3,2,1,0:T(8,128)(2,1)S(1)} %copy-done, bf16[1,128,32,128]{3,2,1,0:T(8,128)(2,1)S(1)} %copy-done.3), kind=kLoop, calls=%fused_computation.3 | loop fusion | bytes 4194304 | tf_op jit(solution)/shard_map/transpose | solution.py:402
  5.8 0.0 copy-done.4
  5.8 0.0 copy-done.5
  5.8 2.1 %copy_bitcast_fusion = (bf16[32,128,128]{2,1,0:T(8,128)(2,1)}, bf16[32,128,128]{2,1,0:T(8,128)(2,1)}) fusion(bf16[1,128,32,128]{3,2,1,0:T(8,128)(2,1)S(1)} %copy-done.4, bf16[1,128,32,128]{3,2,1,0:T(8,128)(2,1)S(1)} %copy-done.5), kind=kLoop, calls=%fused_computation.1 | loop fusion | bytes 4194304 | tf_op jit(solution)/shard_map/transpose | solution.py:402
  8.0 146.4 %attn_bwd.1 = (bf16[32,128,128]{2,1,0:T(8,128)(2,1)}, bf16[32,128,128]{2,1,0:T(8,128)(2,1)}, bf16[32,128,128]{2,1,0:T(8,128)(2,1)}) custom-call(bf16[32,128,128]{2,1,0:T(8,128)(2,1)} %get-tuple-element.18.qh, bf16[32,128,128]{2,1,0:T(8,128)(2,1)} %get-tuple-element.17.doh, bf16[32,128,128]{2,1,0:T(8,128)(2,1)} %get-tuple-element.16.kh, ...), custom_call_target="tpu_custom_call" | custom-call | tf_op jit(solution)/shard_map/attn_bwd/pallas_call | solution.py:359
  154.4 0.0 copy-start.2
  154.4 3.0 %copy.21 = bf16[1,128,32,128]{3,2,1,0:T(8,128)(2,1)} copy(bf16[1,128,32,128]{3,1,2,0:T(8,128)(2,1)} %bitcast.31) | data formatting | bytes 2097152
  157.4 0.0 copy-done.2
  157.4 0.0 copy-start.1
  157.4 1.6 %copy.22 = bf16[1,128,32,128]{3,2,1,0:T(8,128)(2,1)} copy(bf16[1,128,32,128]{3,1,2,0:T(8,128)(2,1)S(1)} %bitcast.30) | data formatting | bytes 2097152
  159.0 0.0 copy-done.1
  159.0 1.6 %copy.23 = bf16[1,128,32,128]{3,2,1,0:T(8,128)(2,1)} copy(bf16[1,128,32,128]{3,1,2,0:T(8,128)(2,1)S(1)} %bitcast.29) | data formatting | bytes 2097152
Async XLA Ops:
  0.6 2.4 %copy-start.6 = (f32[1,32,128]{2,1,0:T(8,128)S(1)}, f32[1,32,128]{2,1,0:T(8,128)}, u32[]{:S(2)}) copy-start(f32[1,32,128]{2,1,0:T(8,128)} %param.11) | copy-start | bytes 49156
  0.6 3.0 %copy-start = (bf16[1,128,32,128]{3,2,1,0:T(8,128)(2,1)S(1)}, bf16[1,128,32,128]{3,2,1,0:T(8,128)(2,1)}, u32[]{:S(2)}) copy-start(bf16[1,128,32,128]{3,2,1,0:T(8,128)(2,1)} %param.10) | copy-start | bytes 3145732
  0.7 3.0 %copy-start.3 = (bf16[1,128,32,128]{3,2,1,0:T(8,128)(2,1)S(1)}, bf16[1,128,32,128]{3,2,1,0:T(8,128)(2,1)}, u32[]{:S(2)}) copy-start(bf16[1,128,32,128]{3,2,1,0:T(8,128)(2,1)} %param.6) | copy-start | bytes 3145732
  3.7 2.1 %copy-start.4 = (bf16[1,128,32,128]{3,2,1,0:T(8,128)(2,1)S(1)}, bf16[1,128,32,128]{3,2,1,0:T(8,128)(2,1)}, u32[]{:S(2)}) copy-start(bf16[1,128,32,128]{3,2,1,0:T(8,128)(2,1)} %param.8) | copy-start | bytes 3145732
  3.7 2.1 %copy-start.5 = (bf16[1,128,32,128]{3,2,1,0:T(8,128)(2,1)S(1)}, bf16[1,128,32,128]{3,2,1,0:T(8,128)(2,1)}, u32[]{:S(2)}) copy-start(bf16[1,128,32,128]{3,2,1,0:T(8,128)(2,1)} %param.7) | copy-start | bytes 3145732
  154.4 3.0 %copy-start.2 = (bf16[32,128,128]{2,1,0:T(8,128)(2,1)S(1)}, bf16[32,128,128]{2,1,0:T(8,128)(2,1)}, u32[]{:S(2)}) copy-start(bf16[32,128,128]{2,1,0:T(8,128)(2,1)} %get-tuple-element.7) | copy-start | bytes 3145732
  157.4 1.7 %copy-start.1 = (bf16[32,128,128]{2,1,0:T(8,128)(2,1)S(1)}, bf16[32,128,128]{2,1,0:T(8,128)(2,1)}, u32[]{:S(2)}) copy-start(bf16[32,128,128]{2,1,0:T(8,128)(2,1)} %get-tuple-element.8) | copy-start | bytes 3145732

commit v5 on v4

--- a/solution.py
+++ b/solution.py
@@ -18,7 +18,7 @@
 LAG = 4
 
 
-def _kernel(scale, qh, doh, kh, vh, st, out_q, out_k, out_v, qd, kv, qdt, kvt, sb, stb, dq, dkt, dvt, p_s, ds_s, dst_s, dq_rx, dk_rx, dv_rx, stage, send, recv_qd, recv_kv, recv_st, fwd_send, fwd_qd, fwd_kv, fwd_st, x_send, x_dq, x_dk, x_dv, o_send, o_recv):
+def _kernel(scale, qh, doh, kh, vh, oh, lse, out_q, out_k, out_v, qd, kv, qdt, kvt, sb, stb, dq, dkt, dvt, p_s, ds_s, dst_s, dq_rx, dk_rx, dv_rx, stage, do_v, o_v, lse_v, st, load, send, recv_qd, recv_kv, recv_st, fwd_send, fwd_qd, fwd_kv, fwd_st, x_send, x_dq, x_dk, x_dv, o_send, o_recv):
     f32, bf16 = jnp.float32, jnp.bfloat16
     R = qh.shape[1]
     BT = 4 * R
@@ -66,6 +66,20 @@
 
     for dev in (x_peer, c_peer):
         pl.semaphore_signal(barrier, inc=1, device_id=dev, device_id_type=pl.DeviceIdType.MESH)
+
+    loads = [pltpu.make_async_copy(a, b, load.at[i]) for i, (a, b) in enumerate(((doh, do_v), (oh, o_v), (lse, lse_v)))]
+    for c in loads:
+        c.start()
+    for c in loads:
+        c.wait()
+
+    @pl.loop(0, N)
+    def _(n):
+        for h in (2 * n, 2 * n + 1):
+            e = do_v[h].astype(f32) * o_v[h].astype(f32)
+            st[h, 0:1, :] = lse_v[pl.ds(h, 1), :]
+            st[h, 1:2, :] = jnp.sum(e.T, axis=0, keepdims=True)
+
     pl.semaphore_wait(barrier, 2 * N + 1)
 
     def parts(h, m, t):
@@ -351,7 +365,7 @@
     drain(stage.at[pl.ds(0, 2 * N - 1)], o_recv.at[0])
 
 
-def _attention(qh, doh, kh, vh, st, scale):
+def _attention(qh, doh, kh, vh, oh, lse, scale):
     h, r, d = qh.shape
     t = 4 * r * N
     f32, bf16, dma = jnp.float32, jnp.bfloat16, pltpu.SemaphoreType.DMA
@@ -359,7 +373,7 @@
     return pl.pallas_call(
         functools.partial(_kernel, scale),
         out_shape=(jax.ShapeDtypeStruct((h, r, d), bf16),) * 3,
-        in_specs=[hbm] * 5,
+        in_specs=[hbm] * 6,
         out_specs=(hbm,) * 3,
         scratch_shapes=[
             pltpu.VMEM((2, t, d), bf16),
@@ -378,6 +392,11 @@
             pltpu.VMEM((h, d, r), f32),
             pltpu.VMEM((h, d, r), f32),
             pltpu.VMEM((h, 3, r, d), bf16),
+            pltpu.VMEM((h, r, d), bf16),
+            pltpu.VMEM((h, r, d), bf16),
+            pltpu.VMEM((h, r), f32),
+            pltpu.VMEM((h, 2, r), f32),
+            dma((3,)),
             dma((3,)), dma((h,)), dma((h,)), dma((h,)),
             dma((3,)), dma((h,)), dma((h,)), dma((h,)),
             dma((3,)), dma((h,)), dma((h,)), dma((h,)),
@@ -385,7 +404,7 @@
         ],
         compiler_params=pltpu.CompilerParams(collective_id=0, has_side_effects=True, vmem_limit_bytes=63 * 1024 * 1024),
         name='attn_bwd',
-    )(qh, doh, kh, vh, st)
+    )(qh, doh, kh, vh, oh, lse)
 
 
 def solution(mesh):
@@ -395,11 +414,8 @@
     stat = P(None, None, rows)
 
     def body(q, k, v, o, do, lse):
-        f32 = jnp.float32
         scale = q.shape[3] ** -0.5
-        dlt = jnp.sum(do.astype(f32) * o.astype(f32), axis=-1)[0].T
-        st = jnp.stack([lse[0], dlt], axis=1)
-        grads = _attention(*[a[0].transpose(1, 0, 2) for a in (q, do, k, v)], st, scale)
+        grads = _attention(*[a[0].transpose(1, 0, 2) for a in (q, do, k, v, o)], lse[0], scale)
         return tuple(g.transpose(1, 0, 2)[None] for g in grads)
 
     return jax.shard_map(body, mesh=fine, in_specs=(seq, seq, seq, seq, seq, stat), out_specs=(seq, seq, seq), check_vma=False)

time: 161 us -> 158 us (0.981)
  the two profiles are of different devices: /device:TPU:4 before, /device:TPU:120 now
where the time goes in v5:
time: 158 us; the launch traced here: 155 us
  Pallas kernels  141 us (89%)
  local copies, waits for them, and re-layouts  13.3 us (8%)
    pallas_call x1, Pallas kernels, _attention(): pl.pallas_call(functools.partial(_kernel, scale), out_shape=(jax.ShapeDty...  141 us
    unnamed x16, local copies, waits for them, and re-layouts  9.03 us
    transpose x2, local copies, waits for them, and re-layouts, body(): a[0].transpose(1, 0, 2)  4.28 us

profile of v5, /device:TPU:120, one launch (start us, length us, event | category | flops | bytes accessed | tf_op | source)
XLA Modules:
  0.0 155.5 jit_solution(15327079847658875018)
XLA Ops:
  0.6 0.0 copy-start.2
  0.6 0.0 copy-start.3
  0.7 2.7 %copy.22 = bf16[1,128,32,128]{3,1,2,0:T(8,128)(2,1)} copy(bf16[1,128,32,128]{3,2,1,0:T(8,128)(2,1)} %param.6) | data formatting | bytes 2097152 | tf_op args[0]
  3.4 0.0 copy-done.2
  3.4 0.0 copy-done.3
  3.4 0.0 copy-start.4
  3.4 0.0 copy-start.5
  3.4 2.1 %copy_bitcast_fusion.2 = (bf16[32,128,128]{2,1,0:T(8,128)(2,1)}, bf16[32,128,128]{2,1,0:T(8,128)(2,1)}) fusion(bf16[1,128,32,128]{3,2,1,0:T(8,128)(2,1)S(1)} %copy-done.2, bf16[1,128,32,128]{3,2,1,0:T(8,128)(2,1)S(1)} %copy-done.3), kind=kLoop, calls=%fused_computation.2 | loop fusion | bytes 4194304 | tf_op jit(solution)/shard_map/transpose | solution.py:418
  5.5 0.0 copy-done.4
  5.5 0.0 copy-done.5
  5.5 2.2 %copy_bitcast_fusion = (bf16[32,128,128]{2,1,0:T(8,128)(2,1)}, bf16[32,128,128]{2,1,0:T(8,128)(2,1)}) fusion(bf16[1,128,32,128]{3,2,1,0:T(8,128)(2,1)S(1)} %copy-done.4, bf16[1,128,32,128]{3,2,1,0:T(8,128)(2,1)S(1)} %copy-done.5), kind=kLoop, calls=%fused_computation | loop fusion | bytes 4194304 | tf_op jit(solution)/shard_map/transpose | solution.py:418
  7.7 141.5 %attn_bwd.1 = (bf16[32,128,128]{2,1,0:T(8,128)(2,1)}, bf16[32,128,128]{2,1,0:T(8,128)(2,1)}, bf16[32,128,128]{2,1,0:T(8,128)(2,1)}) custom-call(bf16[32,128,128]{2,1,0:T(8,128)(2,1)} %bitcast.31, bf16[32,128,128]{2,1,0:T(8,128)(2,1)} %get-tuple-element.15.doh, bf16[32,128,128]{2,1,0:T(8,128)(2,1)} %get-tuple-element.14.kh, ...), custom_call_target="tpu_custom_call" | custom-call | tf_op jit(solution)/shard_map/attn_bwd/pallas_call | solution.py:373
  149.2 0.0 copy-start.1
  149.2 3.0 %copy.14 = bf16[1,128,32,128]{3,2,1,0:T(8,128)(2,1)} copy(bf16[1,128,32,128]{3,1,2,0:T(8,128)(2,1)} %bitcast.34) | data formatting | bytes 2097152
  152.2 0.0 copy-done.1
  152.2 0.0 copy-start
  152.2 1.6 %copy.15 = bf16[1,128,32,128]{3,2,1,0:T(8,128)(2,1)} copy(bf16[1,128,32,128]{3,1,2,0:T(8,128)(2,1)S(1)} %bitcast.33) | data formatting | bytes 2097152
  153.8 0.0 copy-done
  153.8 1.6 %copy.16 = bf16[1,128,32,128]{3,2,1,0:T(8,128)(2,1)} copy(bf16[1,128,32,128]{3,1,2,0:T(8,128)(2,1)S(1)} %bitcast.32) | data formatting | bytes 2097152
Async XLA Ops:
  0.6 2.8 %copy-start.2 = (bf16[1,128,32,128]{3,2,1,0:T(8,128)(2,1)S(1)}, bf16[1,128,32,128]{3,2,1,0:T(8,128)(2,1)}, u32[]{:S(2)}) copy-start(bf16[1,128,32,128]{3,2,1,0:T(8,128)(2,1)} %param.7) | copy-start | bytes 3145732
  0.6 2.8 %copy-start.3 = (bf16[1,128,32,128]{3,2,1,0:T(8,128)(2,1)S(1)}, bf16[1,128,32,128]{3,2,1,0:T(8,128)(2,1)}, u32[]{:S(2)}) copy-start(bf16[1,128,32,128]{3,2,1,0:T(8,128)(2,1)} %param.10) | copy-start | bytes 3145732
  3.4 2.1 %copy-start.4 = (bf16[1,128,32,128]{3,2,1,0:T(8,128)(2,1)S(1)}, bf16[1,128,32,128]{3,2,1,0:T(8,128)(2,1)}, u32[]{:S(2)}) copy-start(bf16[1,128,32,128]{3,2,1,0:T(8,128)(2,1)} %param.9) | copy-start | bytes 3145732
  3.4 2.1 %copy-start.5 = (bf16[1,128,32,128]{3,2,1,0:T(8,128)(2,1)S(1)}, bf16[1,128,32,128]{3,2,1,0:T(8,128)(2,1)}, u32[]{:S(2)}) copy-start(bf16[1,128,32,128]{3,2,1,0:T(8,128)(2,1)} %param.8) | copy-start | bytes 3145732
  149.2 3.0 %copy-start.1 = (bf16[32,128,128]{2,1,0:T(8,128)(2,1)S(1)}, bf16[32,128,128]{2,1,0:T(8,128)(2,1)}, u32[]{:S(2)}) copy-start(bf16[32,128,128]{2,1,0:T(8,128)(2,1)} %get-tuple-element.7) | copy-start | bytes 3145732
  152.2 1.7 %copy-start = (bf16[32,128,128]{2,1,0:T(8,128)(2,1)S(1)}, bf16[32,128,128]{2,1,0:T(8,128)(2,1)}, u32[]{:S(2)}) copy-start(bf16[32,128,128]{2,1,0:T(8,128)(2,1)} %get-tuple-element.8) | copy-start | bytes 3145732
